TPU v7x, 32 devices: a whole 2x2x4 slice. The times are simulated.
32 devices in a mesh: batch: 2 (over x), col: 4 (over z), row: 4 (over y, core).
Axes of the slice: x: 2, y: 2, z: 4, core: 2. Of those that a mesh axis runs over, the one named last changes fastest.
Arguments:
- mat_blocks: float32 [32768, 128, 32], P(('batch', 'row'), 'col'), parts along dimension 0
Outputs:
- output 1: float32 [32768, 128, 32], P(('batch', 'row'), 'col'), parts along dimension 0
- output 2: float32 [256], P('batch'), parts along dimension 0
- output 3: float32 [8, 32, 32], P('batch'), parts along dimension 0
There are 2 independent parts. A program takes and returns all parts, laid end to end along the dimension named above; each array names one.
All inputs are finite; a program needn't handle non-finite values.
Results may differ from a plain program's by a relative error of at most 0.001.
Values sent between devices are 32-bit elements.
A program may use at most 1 GiB of HBM per device.

v0:
```python
import math
import jax
import jax.numpy as jnp
from jax import lax
from jax.sharding import PartitionSpec as P

PANELS = 4
HIGHEST = lax.Precision.HIGHEST


def mat_dot(left_mat, right_mat):
    return jnp.dot(left_mat, right_mat, precision=HIGHEST, preferred_element_type=jnp.float32)


def mat_einsum(einsum_form, left_mat, right_mat):
    return jnp.einsum(einsum_form, left_mat, right_mat, precision=HIGHEST, preferred_element_type=jnp.float32)


def apply_reflector(panel_work, tau_vec, column, col_idx, pivot_row, row_ids, tail_dots, pivot_line):
    col_ids = jnp.arange(panel_work.shape[1])
    alpha_val = lax.dynamic_index_in_dim(pivot_line, col_idx, keepdims=False)
    norm_val = jnp.sqrt(lax.dynamic_index_in_dim(tail_dots, col_idx, keepdims=False))
    beta_val = jnp.where(alpha_val >= 0.0, -norm_val, norm_val)
    tau_val = (beta_val - alpha_val) / beta_val
    scale_val = 1.0 / (alpha_val - beta_val)
    refl_vec = jnp.where(row_ids > pivot_row, column * scale_val, jnp.where(row_ids == pivot_row, 1.0, 0.0))
    refl_dot = scale_val * (tail_dots - alpha_val * pivot_line) + pivot_line
    refl_dot = jnp.where(col_ids > col_idx, refl_dot, 0.0)
    new_col = jnp.where(row_ids < pivot_row, column, jnp.where(row_ids == pivot_row, beta_val, refl_vec))
    panel_work = jnp.where(col_ids[None, :] == col_idx, new_col[:, None], panel_work - tau_val * refl_vec[:, None] * refl_dot[None, :])
    tau_vec = jnp.where(col_ids == col_idx, tau_val, tau_vec)
    return panel_work, tau_vec


def factor_panel_rows(panel_in, row_base, pivot_base):
    local_rows, block_width = panel_in.shape
    row_ids = row_base + jnp.arange(local_rows)

    def column_step(col_idx, loop_state):
        panel_work, tau_vec = loop_state
        pivot_row = pivot_base + col_idx
        column = lax.dynamic_index_in_dim(panel_work, col_idx, axis=1, keepdims=False)
        tail_col = jnp.where(row_ids >= pivot_row, column, 0.0)
        local_pivot = jnp.clip(pivot_row - row_base, 0, local_rows - 1)
        holds_pivot = (pivot_row >= row_base) & (pivot_row < row_base + local_rows)
        pivot_line = lax.dynamic_index_in_dim(panel_work, local_pivot, axis=0, keepdims=False)
        pivot_line = jnp.where(holds_pivot, pivot_line, 0.0)
        packed = jnp.concatenate([mat_dot(tail_col[None, :], panel_work)[0], pivot_line])
        packed = lax.psum(packed, 'row')
        return apply_reflector(panel_work, tau_vec, column, col_idx, pivot_row, row_ids, packed[:block_width], packed[block_width:])

    return lax.fori_loop(0, block_width, column_step, (panel_in, jnp.zeros((block_width,), jnp.float32)))


def tfactor_from_gram(gram_mat, tau_vec):
    block_width = gram_mat.shape[0]
    col_ids = jnp.arange(block_width)
    step_mat = -tau_vec[:, None] * jnp.where(col_ids[None, :] > col_ids[:, None], gram_mat, 0.0)
    eye_mat = jnp.eye(block_width, dtype=jnp.float32)
    inv_acc = eye_mat + step_mat
    power_mat = step_mat
    for level_num in range(max(1, math.ceil(math.log2(block_width))) - 1):
        power_mat = mat_dot(power_mat, power_mat)
        inv_acc = mat_dot(inv_acc, eye_mat + power_mat)
    return inv_acc * tau_vec[None, :]


def solution(mesh):
    col_count = mesh.shape['col']
    block_spec = P(('batch', 'row'), 'col', None)

    def device_fn(a_local):
        local_rows, local_blocks, block_width = a_local.shape
        col_rank = lax.axis_index('col')
        row_base = lax.axis_index('row') * local_rows
        row_ids = row_base + jnp.arange(local_rows)
        col_ids = jnp.arange(block_width)
        global_ids = jnp.arange(local_blocks) * col_count + col_rank
        tau_list = []
        tfac_list = []
        for panel_idx in range(PANELS):
            owner_col = panel_idx % col_count
            block_pos = panel_idx // col_count
            pivot_ids = panel_idx * block_width + col_ids
            panel_out, tau_vec = factor_panel_rows(a_local[:, block_pos, :], row_base, panel_idx * block_width)
            refl_mat = jnp.where(row_ids[:, None] > pivot_ids[None, :], panel_out, jnp.where(row_ids[:, None] == pivot_ids[None, :], 1.0, 0.0))
            gram_mat = lax.psum(mat_einsum('rk,rj->kj', refl_mat, refl_mat), 'row')
            t_factor = tfactor_from_gram(gram_mat, tau_vec)
            packed = jnp.concatenate([refl_mat, t_factor], axis=0)
            packed = lax.psum(jnp.where(col_rank == owner_col, packed, 0.0), 'col')
            refl_mat = packed[:local_rows]
            t_factor = packed[local_rows:]
            w_summed = lax.psum(mat_einsum('rk,rbc->kbc', refl_mat, a_local), 'row')
            w_mat = mat_einsum('kj,kbc->jbc', t_factor, w_summed)
            w_mat = jnp.where((global_ids > panel_idx)[None, :, None], w_mat, 0.0)
            a_local = a_local - mat_einsum('rj,jbc->rbc', refl_mat, w_mat)
            a_local = jnp.where((global_ids == panel_idx)[None, :, None], panel_out[:, None, :], a_local)
            tau_list.append(jnp.diagonal(t_factor))
            tfac_list.append(t_factor)
        return a_local, jnp.concatenate(tau_list), jnp.stack(tfac_list)

    return jax.shard_map(device_fn, mesh=mesh, in_specs=(block_spec,), out_specs=(block_spec, P('batch'), P('batch', None, None)), check_vma=False)
```

profile of v0, /device:TPU:0, one launch (start us, length us, event | category | flops | bytes accessed | tf_op | source)
XLA Modules:
  0.0 2195.2 jit_solution(16483239490666292462)
XLA Ops:
  8.3 381.6 %while.76 = (s32[]{:T(128)}, f32[4096,32]{0,1:T(8,128)S(1)}, f32[32]{0:T(128)S(1)}, s32[]{:T(128)}, s32[]{:T(128)}, /*index=5*/s32[]{:T(128)}, s32[]{:T(128)}, s32[]{:T(128)}, f32[]{:T(128)}, f32[]{:T(128)}) while((s32[]{:T(128)}, f32[4096,32]{0,1:T(8,128)S(1)}, f32[32]{0:T(128)S(1)}, s32[]{:T(128)}, ...), condition=%wide.region_2.3_spmd.clone.clone.clone, body=%wide.region_0.2_spmd.clone.clone.clone.sunk | while | flops 2023920 | bytes 1764387 | solution.py:52
  9.2 8.4 psum.160
  58.4 6.4 psum.160
  82.3 6.2 psum.160
  129.4 6.5 psum.160
  200.7 6.2 psum.160
  355.0 6.2 psum.160
  390.6 10.1 psum.132
  403.0 39.9 %all-reduce.9.cloned.1.call-done = f32[4128,32]{0,1:T(8,128)} async-done(((f32[4128,32]{0,1:T(8,128)}), f32[4128,32]{0,1:T(8,128)}) %all-reduce.9.cloned.1.call-update) | async-done | bytes 528400 | tf_op jit(solution)/shard_map/psum | solution.py:90
  443.0 41.3 %fusion.38 = f32[32,32,32]{2,0,1:T(8,128)} fusion(f32[4096,32,32]{0,2,1:T(8,128)} %param.9, f32[4128,32]{0,1:T(8,128)} %all-reduce.9.cloned.1.call-done), kind=kOutput, calls=%fused_computation.117 | convolution fusion | flops 1610612736 | bytes 17432576 | tf_op jit(solution)/shard_map/rk,rbc->kbc/dot_general | solution.py:16
  484.6 33.1 %all-reduce.11.cloned.1.call-done = f32[32,32,32]{2,0,1:T(8,128)} async-done(((f32[32,32,32]{2,0,1:T(8,128)}), f32[32,32,32]{2,0,1:T(8,128)}) %all-reduce.11.cloned.1.call-update) | async-done | bytes 131088 | tf_op jit(solution)/shard_map/psum | solution.py:93
  519.5 16.1 fusion.49
  535.6 11.8 subtract_select_fusion.7
  553.5 383.8 %while.77 = (s32[]{:T(128)}, f32[4096,32]{0,1:T(8,128)S(1)}, f32[32]{0:T(128)S(1)}, s32[]{:T(128)}, s32[]{:T(128)}, /*index=5*/s32[]{:T(128)}, s32[]{:T(128)}, s...) while((s32[]{:T(128)}, f32[4096,32]{0,1:T(8,128)S(1)}, f32[32]{0:T(128)S(1)}, ...), condition=%wide.region_8.9_spmd.clone.clone.clone, body=%wide.region_6.8_spmd.clone.clone.clone.sunk | while | flops 2023921 | bytes 1764407 | solution.py:52
  589.7 6.4 psum.161
  614.0 6.2 psum.161
  661.7 6.5 psum.161
  733.9 6.2 psum.161
  938.1 10.3 psum.135
  951.1 40.3 %all-reduce.13.cloned.1.call-done = f32[4128,32]{0,1:T(8,128)} async-done(((f32[4128,32]{0,1:T(8,128)}), f32[4128,32]{0,1:T(8,128)}) %all-reduce.13.cloned.1.call-update) | async-done | bytes 528400 | tf_op jit(solution)/shard_map/psum | solution.py:90
  991.5 41.3 %fusion.36 = f32[32,32,32]{2,0,1:T(8,128)} fusion(f32[4096,32,32]{0,2,1:T(8,128)} %copy-done.1, f32[4128,32]{0,1:T(8,128)} %all-reduce.13.cloned.1.call-done), kind=kOutput, calls=%fused_computation.115 | convolution fusion | flops 1610612736 | bytes 17432576 | tf_op jit(solution)/shard_map/rk,rbc->kbc/dot_general | solution.py:16
  1033.4 32.8 %all-reduce.15.cloned.1.call-done = f32[32,32,32]{2,0,1:T(8,128)} async-done(((f32[32,32,32]{2,0,1:T(8,128)}), f32[32,32,32]{2,0,1:T(8,128)}) %all-reduce.15.cloned.1.call-update) | async-done | bytes 131088 | tf_op jit(solution)/shard_map/psum | solution.py:93
  1068.0 16.0 fusion.46
  1084.0 11.8 subtract_select_fusion.6
  1102.0 383.8 %while.78 = (s32[]{:T(128)}, f32[4096,32]{0,1:T(8,128)S(1)}, f32[32]{0:T(128)S(1)}, s32[]{:T(128)}, s32[]{:T(128)}, /*index=5*/s32[]{:T(128)}, s32[]{:T(128)}, s...) while((s32[]{:T(128)}, f32[4096,32]{0,1:T(8,128)S(1)}, ...), condition=%wide.region_14.15_spmd.clone.clone.clone, body=%wide.region_12.14_spmd.clone.clone.clone.sunk | while | flops 2023921 | bytes 1764407 | solution.py:52
  1138.1 6.4 psum.162
  1162.4 6.2 psum.162
  1210.1 6.5 psum.162
  1282.3 6.2 psum.162
  1438.7 6.2 psum.162
  1486.5 10.3 psum.138
  1499.4 40.1 %all-reduce.17.cloned.1.call-done = f32[4128,32]{0,1:T(8,128)} async-done(((f32[4128,32]{0,1:T(8,128)}), f32[4128,32]{0,1:T(8,128)}) %all-reduce.17.cloned.1.call-update) | async-done | bytes 528400 | tf_op jit(solution)/shard_map/psum | solution.py:90
  1539.5 41.3 %fusion.34 = f32[32,32,32]{2,0,1:T(8,128)} fusion(f32[4096,32,32]{0,2,1:T(8,128)} %copy-done.2, f32[4128,32]{0,1:T(8,128)} %all-reduce.17.cloned.1.call-done), kind=kOutput, calls=%fused_computation.113 | convolution fusion | flops 1610612736 | bytes 17432576 | tf_op jit(solution)/shard_map/rk,rbc->kbc/dot_general | solution.py:16
  1581.1 33.1 %all-reduce.19.cloned.1.call-done = f32[32,32,32]{2,0,1:T(8,128)} async-done(((f32[32,32,32]{2,0,1:T(8,128)}), f32[32,32,32]{2,0,1:T(8,128)}) %all-reduce.19.cloned.1.call-update) | async-done | bytes 131088 | tf_op jit(solution)/shard_map/psum | solution.py:93
  1616.0 16.0 fusion.43
  1632.0 11.8 subtract_select_fusion.5
  1650.0 378.7 %while.79 = (s32[]{:T(128)}, f32[4096,32]{0,1:T(8,128)S(1)}, f32[32]{0:T(128)S(1)}, s32[]{:T(128)}, s32[]{:T(128)}, /*index=5*/s32[]{:T(128)}, s32[]{:T(128)}, s...) while((s32[]{:T(128)}, f32[4096,32]{0,1:T(8,128)S(1)}, ...), condition=%wide.region_20.21_spmd.clone.clone.clone, body=%wide.region_18.20_spmd.clone.clone.clone.sunk | while | flops 2023921 | bytes 1764407 | solution.py:52
  1685.7 6.4 psum.163
  1709.6 6.2 psum.163
  1756.8 6.5 psum.163
  1828.0 6.2 psum.163
  1982.3 6.2 psum.163
  2029.5 10.3 psum.141
  2044.5 38.3 %all-reduce.21.cloned.1.call-done = f32[4128,32]{0,1:T(8,128)} async-done(((f32[4128,32]{0,1:T(8,128)}), f32[4128,32]{0,1:T(8,128)}) %all-reduce.21.cloned.1.call-update) | async-done | bytes 528400 | tf_op jit(solution)/shard_map/psum | solution.py:90
  2085.0 41.7 %fusion.32 = f32[32,32,32]{2,0,1:T(8,128)} fusion(f32[4096,32,32]{0,2,1:T(8,128)} %copy-done, f32[4128,32]{0,1:T(8,128)} %all-reduce.21.cloned.1.call-done), kind=kOutput, calls=%fused_computation.111 | convolution fusion | flops 1610612736 | bytes 17432576 | tf_op jit(solution)/shard_map/rk,rbc->kbc/dot_general | solution.py:16
  2127.4 32.8 %all-reduce.23.cloned.1.call-done = f32[32,32,32]{2,0,1:T(8,128)} async-done(((f32[32,32,32]{2,0,1:T(8,128)}), f32[32,32,32]{2,0,1:T(8,128)}) %all-reduce.23.cloned.1.call-update) | async-done | bytes 131088 | tf_op jit(solution)/shard_map/psum | solution.py:93
  2162.0 13.7 fusion.40
  2175.7 12.5 subtract_select_fusion.4
  (2018 shorter events, 1083.9 us)
Async XLA Ops:
  7.2 435.8 %all-reduce.9.cloned.1.call-start = ((), (), s32[]{:S(2)}) async-start(), calls=%async_computation | async-start | bytes 1081344 | tf_op jit(solution)/shard_map/psum | solution.py:90
  402.9 114.7 %all-reduce.11.cloned.1.call-start = ((), (), s32[]{:S(2)}) async-start(), calls=%async_computation.1 | async-start | bytes 1048576 | tf_op jit(solution)/shard_map/psum | solution.py:93
  443.0 74.7 %copy-start.3 = (f32[4128,32]{0,1:T(8,128)S(1)}, f32[4128,32]{0,1:T(8,128)}, u32[]{:S(2)}) copy-start(f32[4128,32]{0,1:T(8,128)} %all-reduce.9.cloned.1.call-done) | copy-start | bytes 1585156
  484.2 507.2 %all-reduce.13.cloned.1.call-start = ((), (), s32[]{:S(2)}) async-start(), calls=%async_computation.2 | async-start | bytes 1081344 | tf_op jit(solution)/shard_map/psum | solution.py:90
  547.3 6.2 copy-start.1
  950.7 115.5 %all-reduce.15.cloned.1.call-start = ((), (), s32[]{:S(2)}) async-start(), calls=%async_computation.3 | async-start | bytes 1048576 | tf_op jit(solution)/shard_map/psum | solution.py:93
  991.5 74.7 %copy-start.4 = (f32[4128,32]{0,1:T(8,128)S(1)}, f32[4128,32]{0,1:T(8,128)}, u32[]{:S(2)}) copy-start(f32[4128,32]{0,1:T(8,128)} %all-reduce.13.cloned.1.call-done) | copy-start | bytes 1585156
  1032.8 506.7 %all-reduce.17.cloned.1.call-start = ((), (), s32[]{:S(2)}) async-start(), calls=%async_computation.4 | async-start | bytes 1081344 | tf_op jit(solution)/shard_map/psum | solution.py:90
  1095.8 6.2 copy-start.2
  1499.1 115.1 %all-reduce.19.cloned.1.call-start = ((), (), s32[]{:S(2)}) async-start(), calls=%async_computation.5 | async-start | bytes 1048576 | tf_op jit(solution)/shard_map/psum | solution.py:93
  1539.5 74.7 %copy-start.5 = (f32[4128,32]{0,1:T(8,128)S(1)}, f32[4128,32]{0,1:T(8,128)}, u32[]{:S(2)}) copy-start(f32[4128,32]{0,1:T(8,128)} %all-reduce.17.cloned.1.call-done) | copy-start | bytes 1585156
  1580.8 502.0 %all-reduce.21.cloned.1.call-start = ((), (), s32[]{:S(2)}) async-start(), calls=%async_computation.6 | async-start | bytes 1081344 | tf_op jit(solution)/shard_map/psum | solution.py:90
  1643.8 6.2 copy-start
  2042.1 118.1 %all-reduce.23.cloned.1.call-start = ((), (), s32[]{:S(2)}) async-start(), calls=%async_computation.7 | async-start | bytes 1048576 | tf_op jit(solution)/shard_map/psum | solution.py:93
  2085.0 75.2 %copy-start.6 = (f32[4128,32]{0,1:T(8,128)S(1)}, f32[4128,32]{0,1:T(8,128)}, u32[]{:S(2)}) copy-start(f32[4128,32]{0,1:T(8,128)} %all-reduce.21.cloned.1.call-done) | copy-start | bytes 1585156
Sparse Core Ops, SparseCore 0:
  403.1 39.8 all-reduce.8
  484.4 33.2 all-reduce.10
  950.8 40.6 all-reduce.12
  1032.9 33.2 all-reduce.14
  1499.2 40.2 all-reduce.16
  1580.9 33.2 all-reduce.18
  2042.2 40.6 all-reduce.20
  2126.9 33.2 all-reduce.22
where the time goes:
time: 2210 us; the launch traced here: 2200 us
  blocking collectives  804 us (36%)
  loops' own time  361 us (16%)
  matrix products  307 us (14%)
  waiting for transfers between devices  291 us (13%)
  other arithmetic  224 us (10%)
  local copies, waits for them, and re-layouts  192 us (9%)
    psum x128, blocking collectives, column_step(): packed = lax.psum(packed, 'row')  763 us
    another operation x4, loops' own time, factor_panel_rows(): lax.fori_loop(0, block_width, column_step, (panel_in, jnp.zeros((block_wi...  361 us
    dot_general x12, matrix products, mat_einsum(): jnp.einsum(einsum_form, left_mat, right_mat, precision=HIGHEST, preferred...  174 us
    psum x4, waiting for transfers between devices, device_fn(): packed = lax.psum(jnp.where(col_rank == owner_col, packed, 0.0), 'col')  159 us
    psum x4, waiting for transfers between devices, device_fn(): w_summed = lax.psum(mat_einsum('rk,rbc->kbc', refl_mat, a_local), 'row')  132 us
    select_n x128, other arithmetic, apply_reflector(): refl_dot = jnp.where(col_ids > col_idx, refl_dot, 0.0)  95.3 us
    dynamic_slice x128, local copies, waits for them, and re-layouts, apply_reflector(): alpha_val = lax.dynamic_index_in_dim(pivot_line, col_idx, keepdims=False)  80.5 us
    dynamic_slice x128, local copies, waits for them, and re-layouts, apply_reflector(): lax.dynamic_index_in_dim(tail_dots, col_idx, keepdims=False)  74.1 us
  transfers between devices with their start and end apart: 8, of which 8 were waited for; matrix products, arithmetic and copies ran while one was open for 0% of the time, Pallas kernels for 0%

commit v1 on v0

v1 whole, which is shorter than its diff:
```python
import functools
import jax
import jax.numpy as jnp
from jax import lax
from jax.experimental import pallas as pl
from jax.experimental.pallas import tpu as pltpu
from jax.sharding import PartitionSpec as P

PANELS = 4
BW = 32
NC = PANELS * BW
HIGHEST = lax.Precision.HIGHEST


def dot_nn(x, y):
    return lax.dot_general(x, y, (((1,), (0,)), ((), ())), precision=HIGHEST, preferred_element_type=jnp.float32)


def dot_nt(x, y):
    return lax.dot_general(x, y, (((1,), (1,)), ((), ())), precision=HIGHEST, preferred_element_type=jnp.float32)


def dot_tn(x, y):
    return lax.dot_general(x, y, (((0,), (0,)), ((), ())), precision=HIGHEST, preferred_element_type=jnp.float32)


def factor_kernel(g_ref, b_ref, face_ref, tfull_ref, tau_ref, rit_ref, nmat_ref, uit_ref, u_ref, li_ref):
    nt = NC // 8
    lane = lax.broadcasted_iota(jnp.int32, (8, NC), 1)
    sub = lax.broadcasted_iota(jnp.int32, (8, NC), 0)

    def row_of(tile, s):
        return jnp.broadcast_to(tile[s:s + 1, :], (8, NC))

    def col_of(tile, k):
        return jnp.broadcast_to(tile[:, k:k + 1], (8, NC))

    g = [g_ref[8 * t:8 * t + 8, :] for t in range(nt)]
    b = [b_ref[8 * t:8 * t + 8, :] for t in range(nt)]
    ri = [jnp.where(lane == sub + 8 * t, 1.0, 0.0) for t in range(nt)]
    li = [jnp.where(lane == sub + 8 * t, 1.0, 0.0) for t in range(nt)]
    inv_row = jnp.zeros((8, NC), jnp.float32)
    tau_row = jnp.zeros((8, NC), jnp.float32)
    invs = []
    for k in range(NC):
        t0, s = divmod(k, 8)
        gcol = [col_of(g[t], k) for t in range(t0, nt)]
        bcol = [col_of(b[t], k) for t in range(t0, nt)]
        diag = row_of(gcol[0], s)
        rs = lax.rsqrt(diag)
        rrow = jnp.where(lane >= k, row_of(g[t0], s) * rs, 0.0)
        rirow = row_of(ri[t0], s) * rs
        for t in range(t0, nt):
            f = gcol[t - t0] * rs
            g[t] = g[t] - f * rrow
            ri[t] = ri[t] - f * rirow
        norm = diag * rs
        alpha = row_of(bcol[0], s)
        sgn = jnp.where(alpha >= 0.0, 1.0, -1.0)
        beta = -sgn * norm
        rsig = -sgn * rrow
        brow = row_of(b[t0], s)
        urow = jnp.where(lane >= k, brow - rsig, 0.0)
        piv = alpha - beta
        inv = 1.0 / piv
        tau_row = jnp.where(lane == k, (beta - alpha) / beta, tau_row)
        lrow = brow * inv_row
        inv_row = jnp.where(lane == k, inv, inv_row)
        uupd = jnp.where(lane > k, urow, 0.0)
        lirow = row_of(li[t0], s)
        for t in range(t0, nt):
            f = bcol[t - t0] * inv
            b[t] = b[t] - f * uupd
            li[t] = li[t] - f * lirow
        face_ref[k:k + 1, :] = jnp.where(lane >= k, rsig, lrow)[0:1]
        u_ref[k:k + 1, :] = urow[0:1]
        rit_ref[k:k + 1, :] = (-sgn * rirow)[0:1]
        li_ref[k:k + 1, :] = lirow[0:1]
        invs.append(inv)
    tau_ref[...] = tau_row
    umat = u_ref[...]
    ut = umat.T
    u_t = [ut[8 * t:8 * t + 8, :] for t in range(nt)]
    e = [jnp.where(lane == sub + 8 * t, 1.0, 0.0) for t in range(nt)]
    for k in range(NC):
        t0, s = divmod(k, 8)
        yrow = row_of(e[t0], s) * invs[k]
        uit_ref[k:k + 1, :] = yrow[0:1]
        for t in range(t0, nt):
            e[t] = e[t] - col_of(u_t[t], k) * yrow
    limat = li_ref[...]
    nmat_ref[...] = dot_tn(limat, uit_ref[...])
    tful = -dot_nt(dot_nt(umat, rit_ref[...]), limat)
    rows = lax.broadcasted_iota(jnp.int32, (NC, NC), 0)
    cols = lax.broadcasted_iota(jnp.int32, (NC, NC), 1)
    tful = jnp.where(cols > rows, tful, 0.0)
    tfull_ref[...] = jnp.where(cols == rows, jnp.broadcast_to(tau_row[0:1], (NC, NC)), tful)


def factor(gram, top):
    sq = jax.ShapeDtypeStruct((NC, NC), jnp.float32)
    return pl.pallas_call(
        factor_kernel,
        out_shape=(sq, sq, jax.ShapeDtypeStruct((8, NC), jnp.float32), sq, sq, sq),
        in_specs=[pl.BlockSpec(memory_space=pltpu.VMEM)] * 2,
        out_specs=tuple([pl.BlockSpec(memory_space=pltpu.VMEM)] * 6),
        scratch_shapes=[pltpu.VMEM((NC, NC), jnp.float32), pltpu.VMEM((NC, NC), jnp.float32)],
        name="factor",
    )(gram, top)


def solution(mesh):
    block_spec = P(('batch', 'row'), 'col', None)

    def device_fn(a_local):
        local_rows, local_blocks, bw = a_local.shape
        ncol = local_blocks * bw
        at = a_local.transpose(1, 2, 0).reshape(ncol, local_rows)
        col_rank = lax.axis_index('col')
        row_rank = lax.axis_index('row')
        pt = lax.all_gather(at[:bw], 'col', axis=0, tiled=True)
        xt = dot_nt(at, pt)
        gram = dot_nt(pt, pt)
        head = jnp.where(row_rank == 0, at[:, :NC], 0.0)
        phead = jnp.where(row_rank == 0, pt[:, :NC].T, 0.0)
        packed = lax.psum(jnp.concatenate([xt, head, gram, phead], axis=0), 'row')
        xt = packed[:ncol]
        head = packed[ncol:2 * ncol]
        gram = packed[2 * ncol:2 * ncol + NC]
        phead = packed[2 * ncol + NC:]
        face, tfull, tau8, rit, nmat, uit = factor(gram, phead)
        r12t = dot_nt(xt, rit)
        zt = dot_nn(head - r12t, nmat)
        own = lax.dynamic_slice_in_dim(uit, col_rank * bw, bw, axis=0) if False else None
        uinv_own = lax.dynamic_slice_in_dim(uit.T, col_rank * bw, bw, axis=1).T
        zt = jnp.concatenate([-uinv_own, zt[bw:]], axis=0)
        base = jnp.concatenate([jnp.zeros_like(at[:bw]), at[bw:]], axis=0)
        out = base - dot_nn(zt, pt)
        face_own = lax.dynamic_slice_in_dim(face, col_rank * bw, bw, axis=1).T
        top = jnp.concatenate([face_own, r12t[bw:]], axis=0)
        top = jnp.where(row_rank == 0, top, out[:, :NC])
        out = lax.dynamic_update_slice(out, top, (0, 0))
        a_out = out.reshape(local_blocks, bw, local_rows).transpose(2, 0, 1)
        tfac = jnp.stack([tfull[j * bw:(j + 1) * bw, j * bw:(j + 1) * bw] for j in range(PANELS)])
        return a_out, tau8[0], tfac

    return jax.shard_map(device_fn, mesh=mesh, in_specs=(block_spec,), out_specs=(block_spec, P('batch'), P('batch', None, None)), check_vma=False)
```

time: 2210 us -> 185 us (0.08)
  blocking collectives: 804 us -> 0 us
  loops' own time: 361 us -> 0 us
  matrix products: 307 us -> 39.2 us
  waiting for transfers between devices: 291 us -> 72.6 us
  other arithmetic: 224 us -> 6.29 us
  local copies, waits for them, and re-layouts: 192 us -> 29 us
  Pallas kernels: 0 us -> 22.6 us
    psum x132 -> x0, blocking collectives: 804 us -> none  [the longest x128 763 us: column_step(): packed = lax.psum(packed, 'row')]
    another operation x4 -> x0, loops' own time: 361 us -> none  [factor_panel_rows(): lax.fori_loop(0, block_width, column_step, (panel_in, jnp.zeros((block_wi...]
    psum x8 -> x1, waiting for transfers between devices: 290 us -> 25.1 us  [device_fn(): packed = lax.psum(jnp.concatenate([xt, head, gram, phead], axis=0), 'row')]
    select_n x652 -> x2, other arithmetic: 209 us -> 1.09 us  [the longest x1 1.08 us: device_fn(): head = jnp.where(row_rank == 0, at[:, :NC], 0.0)]
    dot_general x172 -> x5, matrix products: 245 us -> 39.2 us  [the longest x3 21.3 us: dot_nt(): lax.dot_general(x, y, (((1,), (1,)), ((), ())), precision=HIGHEST, prefer...]
    dynamic_slice x384 -> x0, local copies, waits for them, and re-layouts: 157 us -> none  [the longest x128 80.5 us: apply_reflector(): alpha_val = lax.dynamic_index_in_dim(pivot_line, col_idx, keepdims=False)]
    unnamed x4 -> x0, matrix products: 61.8 us -> none
    all_gather x0 -> x1, waiting for transfers between devices: none -> 47.4 us  [device_fn(): pt = lax.all_gather(at[:bw], 'col', axis=0, tiled=True)]
  transfers between devices with their start and end apart: 8 -> 2, of which waited for: 8 -> 2; matrix products, arithmetic and copies ran while one was open for 0% -> 7% of each run, Pallas kernels for 0% -> 0%
where the time goes in v1:
time: 185 us; the launch traced here: 184 us
  waiting for transfers between devices  72.6 us (39%)
  matrix products  39.2 us (21%)
  local copies, waits for them, and re-layouts  29 us (16%)
  Pallas kernels  22.6 us (12%)
  between operations  14.1 us (8%)
  other arithmetic  6.29 us (3%)
    all_gather x1, waiting for transfers between devices, device_fn(): pt = lax.all_gather(at[:bw], 'col', axis=0, tiled=True)  47.4 us
    psum x1, waiting for transfers between devices, device_fn(): packed = lax.psum(jnp.concatenate([xt, head, gram, phead], axis=0), 'row')  25.1 us
    pallas_call x1, Pallas kernels, factor(): pl.pallas_call(factor_kernel, out_shape=(sq, sq, jax.ShapeDtypeStruct((8,...  22.6 us
    dot_general x3, matrix products, dot_nt(): lax.dot_general(x, y, (((1,), (1,)), ((), ())), precision=HIGHEST, prefer...  21.3 us
    dot_general x2, matrix products, dot_nn(): lax.dot_general(x, y, (((1,), (0,)), ((), ())), precision=HIGHEST, prefer...  17.9 us
    slice x1, local copies, waits for them, and re-layouts, device_fn(): base = jnp.concatenate([jnp.zeros_like(at[:bw]), at[bw:]], axis=0)  11.5 us
    all_gather x1, local copies, waits for them, and re-layouts, device_fn(): pt = lax.all_gather(at[:bw], 'col', axis=0, tiled=True)  5.03 us
    unnamed x4, local copies, waits for them, and re-layouts  3.99 us
  transfers between devices with their start and end apart: 2, of which 2 were waited for; matrix products, arithmetic and copies ran while one was open for 7% of the time, Pallas kernels for 0%

profile of v1, /device:TPU:0, one launch (start us, length us, event | category | flops | bytes accessed | tf_op | source)
XLA Modules:
  0.0 183.9 jit_solution(12358406287367386283)
XLA Ops:
  7.2 0.0 all-gather.3.cloned.1.call-start
  7.2 1.1 slice.74
  8.3 1.3 copy.10
  9.6 0.0 all-gather.3.cloned.1.call-update
  9.6 0.0 all-reduce.3.cloned.1.call-start
  9.7 1.1 slice_select_fusion.1
  10.8 47.4 %all-gather.3.cloned.1.call-done = f32[1,128,4096]{2,0,1:T(1,128)} async-done(((f32[1,32,4096]{2,0,1:T(1,128)}), f32[1,128,4096]{2,0,1:T(1,128)}) %all-gather.3.cloned.1.call-update) | async-done | bytes 2097168 | tf_op jit(solution)/shard_map/all_gather | solution.py:121
  58.2 5.0 %copy.11 = f32[1,128,4096]{1,2,0:T(8,128)S(1)} copy(f32[1,128,4096]{2,0,1:T(1,128)} %all-gather.3.cloned.1.call-done) | data formatting | bytes 4194304 | tf_op jit(solution)/shard_map/all_gather | solution.py:121
  63.2 3.5 %fusion.10 = f32[128,128]{1,0:T(8,128)S(1)} fusion(f32[1,128,4096]{1,2,0:T(8,128)S(1)} %copy.11), kind=kOutput, calls=%fused_computation.24 | convolution fusion | flops 805306368 | bytes 2162688 | tf_op jit(solution)/shard_map/dot_general | solution.py:20
  66.7 16.2 %fusion.12 = f32[1024,128]{1,0:T(8,128)S(1)} fusion(f32[1024,4096]{1,0:T(8,128)} %bitcast.33, f32[1,128,4096]{1,2,0:T(8,128)S(1)} %copy.11), kind=kOutput, calls=%fused_computation.26 | convolution fusion | flops 6442450944 | bytes 19398656 | tf_op jit(solution)/shard_map/dot_general | solution.py:20
  82.9 1.1 pad_maximum_fusion
  84.0 0.0 all-reduce.3.cloned.1.call-update
  84.0 11.5 %slice.73 = f32[31,32,4096]{2,1,0:T(8,128)} slice(f32[32,32,4096]{2,1,0:T(8,128)} %bitcast.34), slice={[1:32], [0:32], [0:4096]} | slice | bytes 32505856 | tf_op jit(solution)/shard_map/slice | solution.py:137
  95.6 25.1 %all-reduce.3.cloned.1.call-done = f32[2304,128]{1,0:T(8,128)} async-done(((f32[2304,128]{1,0:T(8,128)}), f32[2304,128]{1,0:T(8,128)}) %all-reduce.3.cloned.1.call-update) | async-done | bytes 1179664 | tf_op jit(solution)/shard_map/psum | solution.py:126
  120.7 0.0 slice-start
  120.7 1.6 fusion.15
  122.3 22.6 %factor.1 = (f32[128,128]{1,0:T(8,128)}, f32[128,128]{1,0:T(8,128)}, f32[8,128]{1,0:T(8,128)}, f32[128,128]{1,0:T(8,128)}, f32[128,128]{1,0:T(8,128)}, /*index=5*/f32[128,128]{1,0:T(8,128)}) custom-call(f32[128,128]{1,0:T(8,128)} %get-tuple-element.16.g_ref, f32[128,128]{1,0:T(8,128)} %get-tuple-element.15.b_ref), custom_call_target="tpu_custom_call" | custom-call | tf_op jit(solution)/shard_map/factor/pallas_call | solution.py:102
  144.9 0.0 copy-start.1
  144.9 1.2 slice_bitcast_fusion.4
  146.1 0.9 copy.12
  147.0 0.7 dynamic-slice_negate_fusion
  147.8 1.5 slice_bitcast_fusion.3
  149.2 1.6 fusion.1
  150.8 0.8 slice.82
  151.7 0.0 slice-done
  151.7 0.0 copy-done.1
  151.7 0.6 fusion.6
  152.3 17.4 %pad_subtract_fusion = f32[1024,4096]{1,0:T(8,128)S(1)} fusion(f32[992,4096]{1,0:T(8,128)} %bitcast.35, f32[992,128]{1,0:T(8,128)S(1)} %fusion.6, f32[32,128]{1,0:T(8,128)S(1)} %dynamic-slice_negate_fusion, f32[1,128,4096]{1,2,0:T(8,128)S(1)} %copy.11), kind=kOutput, calls=%fused_computation | convolution fusion | flops 6446776320 | bytes 35651584 | tf_op jit(solution)/shard_map/dot_general | solution.py:16
  169.7 1.2 fusion
  170.8 0.0 copy-start
  170.8 2.2 %pad_maximum_fusion.1 = f32[4,32,32]{2,1,0:T(8,128)} fusion(f32[1,32,32]{2,1,0:T(8,128)} %get-tuple-element.18, f32[1,32,32]{2,1,0:T(8,128)} %get-tuple-element.19, f32[1,32,32]{2,1,0:T(8,128)} %get-tuple-element.20, f32[1,32,32]{2,1,0:T(8,128)} %get-tuple-element.17), kind=kLoop, calls=%fused_computation.14 | loop fusion | flops 12288 | bytes 32768 | tf_op jit(solution)/shard_map/stack | solution.py:144
  173.0 4.0 %copy-done = f32[1024,4096]{1,0:T(8,128)} copy-done((f32[1024,4096]{1,0:T(8,128)}, f32[1024,4096]{1,0:T(8,128)S(1)}, u32[]{:S(2)}) %copy-start) | copy-done | bytes 16777240
  (2 shorter events, 0.0 us)
Async XLA Ops:
  7.2 51.0 %all-gather.3.cloned.1.call-start = ((), (), s32[]{:S(2)}) async-start(), calls=%async_computation.1 | async-start | bytes 2621440 | tf_op jit(solution)/shard_map/all_gather | solution.py:121
  9.6 111.1 %all-reduce.3.cloned.1.call-start = ((), (), s32[]{:S(2)}) async-start(), calls=%async_computation | async-start | bytes 2359296 | tf_op jit(solution)/shard_map/psum | solution.py:126
  120.7 31.0 %slice-start = ((f32[2304,128]{1,0:T(8,128)}), f32[1024,128]{1,0:T(8,128)S(1)}, s32[]{:S(2)}) async-start(f32[2304,128]{1,0:T(8,128)} %all-reduce.3.cloned.1.call-done), calls=%async_computation.2 | async-start | bytes 1048576 | tf_op jit(solution)/shard_map/slice | solution.py:128
  144.9 6.8 %copy-start.1 = (f32[128,128]{1,0:T(8,128)S(1)}, f32[128,128]{1,0:T(8,128)}, u32[]{:S(2)}) copy-start(f32[128,128]{1,0:T(8,128)} %get-tuple-element.11) | copy-start | bytes 196612
  170.8 6.2 %copy-start = (f32[1024,4096]{1,0:T(8,128)}, f32[1024,4096]{1,0:T(8,128)S(1)}, u32[]{:S(2)}) copy-start(f32[1024,4096]{1,0:T(8,128)S(1)} %fusion) | copy-start | bytes 50331652
Sparse Core Ops, SparseCore 0:
  10.1 48.0 all-gather.2
  84.2 36.4 all-reduce.2

commit v2 on v1

v2 whole, which is shorter than its diff:
```python
import functools
import jax
import jax.numpy as jnp
from jax import lax
from jax.experimental import pallas as pl
from jax.experimental.pallas import tpu as pltpu
from jax.sharding import PartitionSpec as P

PANELS = 4
BW = 32
NC = PANELS * BW
CH = 512
HIGHEST = lax.Precision.HIGHEST
MESH = pl.DeviceIdType.MESH


def dot_nn(x, y):
    return lax.dot_general(x, y, (((1,), (0,)), ((), ())), precision=HIGHEST, preferred_element_type=jnp.float32)


def dot_nt(x, y):
    return lax.dot_general(x, y, (((1,), (1,)), ((), ())), precision=HIGHEST, preferred_element_type=jnp.float32)


def dot_tn(x, y):
    return lax.dot_general(x, y, (((0,), (0,)), ((), ())), precision=HIGHEST, preferred_element_type=jnp.float32)


def factor_kernel(g_ref, ptop_ref, facet_ref, tfac_ref, tau_ref, rit_ref, nmat_ref, uit_ref, u_ref, li_ref, face_ref):
    nt = NC // 8
    lane = lax.broadcasted_iota(jnp.int32, (8, NC), 1)
    sub = lax.broadcasted_iota(jnp.int32, (8, NC), 0)

    def row_of(tile, s):
        return jnp.broadcast_to(tile[s:s + 1, :], (8, NC))

    def col_of(tile, k):
        return jnp.broadcast_to(tile[:, k:k + 1], (8, NC))

    g = [g_ref[8 * t:8 * t + 8, :] for t in range(nt)]
    top = ptop_ref[...].T
    b = [top[8 * t:8 * t + 8, :] for t in range(nt)]
    ri = [jnp.where(lane == sub + 8 * t, 1.0, 0.0) for t in range(nt)]
    li = [jnp.where(lane == sub + 8 * t, 1.0, 0.0) for t in range(nt)]
    inv_row = jnp.zeros((8, NC), jnp.float32)
    tau_row = jnp.zeros((8, NC), jnp.float32)
    invs = []
    for k in range(NC):
        t0, s = divmod(k, 8)
        gcol = [col_of(g[t], k) for t in range(t0, nt)]
        bcol = [col_of(b[t], k) for t in range(t0, nt)]
        diag = row_of(gcol[0], s)
        rs = lax.rsqrt(diag)
        rrow = jnp.where(lane >= k, row_of(g[t0], s) * rs, 0.0)
        rirow = row_of(ri[t0], s) * rs
        for t in range(t0, nt):
            f = gcol[t - t0] * rs
            g[t] = g[t] - f * rrow
            ri[t] = ri[t] - f * rirow
        norm = diag * rs
        alpha = row_of(bcol[0], s)
        sgn = jnp.where(alpha >= 0.0, 1.0, -1.0)
        beta = -sgn * norm
        rsig = -sgn * rrow
        brow = row_of(b[t0], s)
        urow = jnp.where(lane >= k, brow - rsig, 0.0)
        piv = alpha - beta
        inv = 1.0 / piv
        tau_row = jnp.where(lane == k, (beta - alpha) / beta, tau_row)
        lrow = brow * inv_row
        inv_row = jnp.where(lane == k, inv, inv_row)
        uupd = jnp.where(lane > k, urow, 0.0)
        lirow = row_of(li[t0], s)
        for t in range(t0, nt):
            f = bcol[t - t0] * inv
            b[t] = b[t] - f * uupd
            li[t] = li[t] - f * lirow
        face_ref[k:k + 1, :] = jnp.where(lane >= k, rsig, lrow)[0:1]
        u_ref[k:k + 1, :] = urow[0:1]
        rit_ref[k:k + 1, :] = (-sgn * rirow)[0:1]
        li_ref[k:k + 1, :] = lirow[0:1]
        invs.append(inv)
    tau_ref[...] = tau_row[0:1]
    facet_ref[...] = face_ref[...].T
    umat = u_ref[...]
    ut = umat.T
    u_t = [ut[8 * t:8 * t + 8, :] for t in range(nt)]
    e = [jnp.where(lane == sub + 8 * t, 1.0, 0.0) for t in range(nt)]
    for k in range(NC):
        t0, s = divmod(k, 8)
        yrow = row_of(e[t0], s) * invs[k]
        uit_ref[k:k + 1, :] = yrow[0:1]
        for t in range(t0, nt):
            e[t] = e[t] - col_of(u_t[t], k) * yrow
    limat = li_ref[...]
    nmat_ref[...] = dot_tn(limat, uit_ref[...])
    tful = -dot_nt(dot_nt(umat, rit_ref[...]), limat)
    rows = lax.broadcasted_iota(jnp.int32, (NC, NC), 0)
    cols = lax.broadcasted_iota(jnp.int32, (NC, NC), 1)
    tful = jnp.where(cols > rows, tful, 0.0)
    tful = jnp.where(cols == rows, jnp.broadcast_to(tau_row[0:1], (NC, NC)), tful)
    for j in range(PANELS):
        tfac_ref[j] = tful[j * BW:(j + 1) * BW, j * BW:(j + 1) * BW]


def factor(gram, ptop):
    sq = jax.ShapeDtypeStruct((NC, NC), jnp.float32)
    return pl.pallas_call(
        factor_kernel,
        out_shape=(sq, jax.ShapeDtypeStruct((PANELS, BW, BW), jnp.float32), jax.ShapeDtypeStruct((1, NC), jnp.float32), sq, sq, sq),
        in_specs=[pl.BlockSpec(memory_space=pltpu.VMEM)] * 2,
        out_specs=tuple([pl.BlockSpec(memory_space=pltpu.VMEM)] * 6),
        scratch_shapes=[pltpu.VMEM((NC, NC), jnp.float32)] * 3,
        cost_estimate=pl.CostEstimate(flops=400_000_000, bytes_accessed=600_000, transcendentals=0),
        name="factor",
    )(gram, ptop)


def gather_kernel(at_ref, pt_out, xh_out, g_out, ptop_out, head_out,
                  a_v, pt_v, x_v, g_v, g_in, x_in, head_v, ptop_v,
                  a_sem, own_sem, send_r, send_l, recv, h_sem, hsend, hrecv, psend, precv, gsend, grecv, xsend, xrecv, out_sem):
    ncol, local_rows = at_ref.shape
    nch = local_rows // CH
    half = ncol // 2
    q = lax.axis_index('col')
    r = lax.axis_index('row')
    last = lax.axis_size('col') - 1

    def own_load(c):
        return pltpu.make_async_copy(at_ref.at[pl.ds(0, BW), pl.ds(c * CH, CH)], pt_v.at[c, q], own_sem.at[c])

    def a_load(c):
        return pltpu.make_async_copy(at_ref.at[:, pl.ds(c * CH, CH)], a_v.at[c], a_sem.at[c])

    def pt_store(c):
        return pltpu.make_async_copy(pt_v.at[c], pt_out.at[:, :, pl.ds(c * CH, CH)], out_sem.at[c])

    def hop(c, j, to, sems):
        return pltpu.make_async_remote_copy(
            src_ref=pt_v.at[c, j], dst_ref=pt_v.at[c, j], send_sem=sems.at[c, j], recv_sem=recv.at[c, j],
            device_id={'col': to}, device_id_type=MESH)

    def head_send(p):
        return pltpu.make_async_remote_copy(
            src_ref=at_ref.at[:, pl.ds(0, NC)], dst_ref=head_v, send_sem=hsend.at[p], recv_sem=hrecv,
            device_id={'row': p}, device_id_type=MESH)

    def ptop_send(p):
        return pltpu.make_async_remote_copy(
            src_ref=pt_v.at[0, :, :, pl.ds(0, NC)], dst_ref=ptop_v, send_sem=psend.at[p], recv_sem=precv,
            device_id={'row': p}, device_id_type=MESH)

    for c in range(nch):
        own_load(c).start()
    for c in range(nch):
        a_load(c).start()

    barrier = pltpu.get_barrier_semaphore()

    @pl.when(q > 0)
    def _():
        pl.semaphore_signal(barrier, inc=1, device_id={'col': q - 1}, device_id_type=MESH)

    @pl.when(q < last)
    def _():
        pl.semaphore_signal(barrier, inc=1, device_id={'col': q + 1}, device_id_type=MESH)

    for d in range(1, 4):
        pl.semaphore_signal(barrier, inc=1, device_id={'row': (r + d) % 4}, device_id_type=MESH)
    inner = jnp.logical_and(q > 0, q < last)

    @pl.when(inner)
    def _():
        pl.semaphore_wait(barrier, 5)

    @pl.when(jnp.logical_not(inner))
    def _():
        pl.semaphore_wait(barrier, 4)

    for c in range(nch):
        own_load(c).wait()

        @pl.when(q < last)
        def _():
            hop(c, q, q + 1, send_r).start()

        @pl.when(q > 0)
        def _():
            hop(c, q, q - 1, send_l).start()

    head_local = pltpu.make_async_copy(at_ref.at[:, pl.ds(0, NC)], head_v, h_sem)

    @pl.when(r == 0)
    def _():
        for p in range(1, 4):
            head_send(p).start()
        head_local.start()

    x_v[...] = jnp.zeros_like(x_v)
    g_v[...] = jnp.zeros_like(g_v)

    def chunk(c, carry):
        for d in range(1, 4):
            @pl.when(q >= d)
            def _():
                hop(c, q - d, q, send_r).wait_recv()

                @pl.when(q < last)
                def _():
                    hop(c, q - d, q + 1, send_r).start()

            @pl.when(q + d <= last)
            def _():
                hop(c, q + d, q, send_l).wait_recv()

                @pl.when(q > 0)
                def _():
                    hop(c, q + d, q - 1, send_l).start()

        pt_store(c).start()

        @pl.when(jnp.logical_and(c == 0, r == 0))
        def _():
            for p in range(1, 4):
                ptop_send(p).start()
            for j in range(PANELS):
                ptop_out[j * BW:(j + 1) * BW, :] = pt_v[0, j, :, 0:NC]

        a_load(c).wait()
        p = pt_v[c].reshape(NC, CH)
        x_v[...] += dot_nt(a_v[c], p)
        g_v[...] += dot_nt(p, p)
        return carry

    lax.fori_loop(0, nch, chunk, 0)

    core = r % 2
    mate = r + 1 - 2 * core
    x_copy = pltpu.make_async_remote_copy(
        src_ref=x_v.at[pl.ds(half * (1 - core), half)], dst_ref=x_in, send_sem=xsend, recv_sem=xrecv,
        device_id={'row': mate}, device_id_type=MESH)
    x_copy.start()
    g_copies = []
    for d in range(1, 4):
        g_copies.append(pltpu.make_async_remote_copy(
            src_ref=g_v, dst_ref=g_in.at[d - 1], send_sem=gsend.at[d - 1], recv_sem=grecv.at[d - 1],
            device_id={'row': (r + d) % 4}, device_id_type=MESH))
        g_copies[-1].start()

    @pl.when(r == 0)
    def _():
        for p in range(1, 4):
            head_send(p).wait_send()
            ptop_send(p).wait_send()
        head_local.wait()

    @pl.when(r > 0)
    def _():
        head_send(0).wait_recv()
        ptop_send(0).wait_recv()
        for j in range(PANELS):
            ptop_out[j * BW:(j + 1) * BW, :] = ptop_v[j]

    head_store = pltpu.make_async_copy(head_v, head_out, h_sem)
    head_store.start()

    def drain(c, carry):
        pt_store(c).wait()
        for j in range(PANELS):
            @pl.when(jnp.logical_and(j <= q, q < last))
            def _():
                hop(c, j, q + 1, send_r).wait_send()

            @pl.when(jnp.logical_and(j >= q, q > 0))
            def _():
                hop(c, j, q - 1, send_l).wait_send()
        return carry

    lax.fori_loop(0, nch, drain, 0)
    for g_copy in g_copies:
        g_copy.wait()
    parts = [g_v[...]] + [g_in[d - 1] for d in range(1, 4)]
    total = None
    for row in range(4):
        dist = (r - row + 4) % 4
        part = jnp.where(dist == 0, parts[0], jnp.where(dist == 1, parts[1], jnp.where(dist == 2, parts[2], parts[3])))
        total = part if total is None else total + part
    g_out[...] = total
    x_copy.wait()
    xh_out[...] = x_v[pl.ds(half * core, half), :] + x_in[...]
    head_store.wait()


def gather(at):
    ncol, local_rows = at.shape
    nch = local_rows // CH
    f32 = jnp.float32
    vm, anys = pl.BlockSpec(memory_space=pltpu.VMEM), pl.BlockSpec(memory_space=pl.ANY)
    dma = pltpu.SemaphoreType.DMA
    return pl.pallas_call(
        gather_kernel,
        out_shape=(jax.ShapeDtypeStruct((PANELS, BW, local_rows), f32), jax.ShapeDtypeStruct((ncol // 2, NC), f32),
                   jax.ShapeDtypeStruct((NC, NC), f32), jax.ShapeDtypeStruct((NC, NC), f32), jax.ShapeDtypeStruct((ncol, NC), f32)),
        in_specs=[anys],
        out_specs=(anys, vm, vm, vm, anys),
        scratch_shapes=[pltpu.VMEM((nch, ncol, CH), f32), pltpu.VMEM((nch, PANELS, BW, CH), f32), pltpu.VMEM((ncol, NC), f32),
                        pltpu.VMEM((NC, NC), f32), pltpu.VMEM((3, NC, NC), f32), pltpu.VMEM((ncol // 2, NC), f32),
                        pltpu.VMEM((ncol, NC), f32), pltpu.VMEM((PANELS, BW, NC), f32),
                        dma((nch,)), dma((nch,)), dma((nch, 4)), dma((nch, 4)), dma((nch, 4)), dma, dma((4,)), dma, dma((4,)), dma,
                        dma((3,)), dma((3,)), dma, dma, dma((nch,))],
        compiler_params=pltpu.CompilerParams(collective_id=0, has_side_effects=True, vmem_limit_bytes=48 * 1024 * 1024),
        name="gather",
    )(at)


def split3(x):
    hi = x.astype(jnp.bfloat16)
    rem = x - hi.astype(jnp.float32)
    mid = rem.astype(jnp.bfloat16)
    lo = (rem - mid.astype(jnp.float32)).astype(jnp.bfloat16)
    return hi, mid, lo


def update_kernel(at_ref, pt_ref, x0_ref, x1_ref, x2_ref, x3_ref, head_ref, rit_ref, nmat_ref, uit_ref, facet_ref, out_ref, zhm_v, zhl_v, top_v):
    step = pl.program_id(0)
    q = lax.axis_index('col')
    r = lax.axis_index('row')
    ncol = head_ref.shape[0]
    half = ncol // 2

    @pl.when(step == 0)
    def _():
        core = r % 2
        rit = rit_ref[...]
        nmat = nmat_ref[...]
        mine = pl.multiple_of(half * core, half)
        other = pl.multiple_of(half * (1 - core), half)
        for lo, xa, xb in ((mine, x0_ref, x1_ref), (other, x2_ref, x3_ref)):
            r12t = dot_nt(xa[...] + xb[...], rit)
            top_v[pl.ds(lo, half), :] = r12t
            z = dot_nn(head_ref[pl.ds(lo, half), :] - r12t, nmat)
            zh, zm, zl = split3(z)
            zhm_v[pl.ds(lo, half), 0:NC] = zh
            zhm_v[pl.ds(lo, half), NC:2 * NC] = zm
            zhl_v[pl.ds(lo, half), 0:NC] = zh
            zhl_v[pl.ds(lo, half), NC:2 * NC] = zl
        own = pl.ds(pl.multiple_of(q * BW, BW), BW)
        top_v[0:BW, :] = facet_ref[own, :]
        zh, zm, zl = split3(-uit_ref[own, :])
        zhm_v[0:BW, 0:NC] = zh
        zhm_v[0:BW, NC:2 * NC] = zm
        zhl_v[0:BW, 0:NC] = zh
        zhl_v[0:BW, NC:2 * NC] = zl

    ph, pm, plo = split3(pt_ref[...].reshape(NC, pt_ref.shape[2]))
    w_hm = jnp.concatenate([ph, pm], axis=0)
    w_mh = jnp.concatenate([pm, ph], axis=0)
    w_lh = jnp.concatenate([plo, ph], axis=0)

    def dot16(x, y):
        return lax.dot_general(x, y, (((1,), (0,)), ((), ())), preferred_element_type=jnp.float32)

    zhm = zhm_v[...]
    prod = dot16(zhm, w_hm) + (dot16(zhm, w_mh) + dot16(zhl_v[...], w_lh))
    out_ref[BW:, :] = at_ref[BW:, :] - prod[BW:]
    out_ref[0:BW, :] = -prod[0:BW]

    @pl.when(jnp.logical_and(step == 0, r == 0))
    def _():
        out_ref[:, 0:NC] = top_v[...]


def update(at, pt, xs, head, rit, nmat, uit, facet):
    ncol, local_rows = at.shape
    lanes = 512
    full = lambda a: pl.BlockSpec(a.shape, lambda i: (0,) * a.ndim)
    strip = pl.BlockSpec((ncol, lanes), lambda i: (0, i))
    return pl.pallas_call(
        update_kernel,
        grid=(local_rows // lanes,),
        out_shape=jax.ShapeDtypeStruct(at.shape, jnp.float32),
        in_specs=[strip, pl.BlockSpec((PANELS, BW, lanes), lambda i: (0, 0, i))] + [full(x) for x in xs]
        + [full(head), full(rit), full(nmat), full(uit), full(facet)],
        out_specs=strip,
        scratch_shapes=[pltpu.VMEM((ncol, 2 * NC), jnp.bfloat16), pltpu.VMEM((ncol, 2 * NC), jnp.bfloat16), pltpu.VMEM((ncol, NC), jnp.float32)],
        compiler_params=pltpu.CompilerParams(dimension_semantics=("arbitrary",), vmem_limit_bytes=48 * 1024 * 1024),
        name="update",
    )(at, pt, *xs, head, rit, nmat, uit, facet)


def solution(mesh):
    block_spec = P(('batch', 'row'), 'col', None)

    def device_fn(a_local):
        local_rows, local_blocks, bw = a_local.shape
        ncol = local_blocks * bw
        at = a_local.transpose(1, 2, 0).reshape(ncol, local_rows)
        pt, xh, gram, ptop, head = gather(at)
        x1, x2, x3 = [lax.ppermute(xh, 'row', [(i, i ^ b) for i in range(4)]) for b in (2, 1, 3)]
        facet, tfac, tau, rit, nmat, uit = factor(gram, ptop)
        out = update(at, pt, (xh, x1, x2, x3), head, rit, nmat, uit, facet)
        a_out = out.reshape(local_blocks, bw, local_rows).transpose(2, 0, 1)
        return a_out, tau.reshape(NC), tfac

    return jax.shard_map(device_fn, mesh=mesh, in_specs=(block_spec,), out_specs=(block_spec, P('batch'), P('batch', None, None)), check_vma=False)
```

time: 185 us -> 117 us (0.63)
  Pallas kernels: 22.6 us -> 109 us
  waiting for transfers between devices: 72.6 us -> 0.01 us
  matrix products: 39.2 us -> 0 us
  local copies, waits for them, and re-layouts: 29 us -> 4.6 us
  between operations: 14.1 us -> 0.67 us
  other arithmetic: 6.29 us -> 0 us
  starting transfers between devices: 0.08 us -> 2.15 us
    pallas_call x1 -> x3, Pallas kernels: 22.6 us -> 109 us  [the longest x1 66.9 us: gather(): pl.pallas_call(gather_kernel, out_shape=(jax.ShapeDtypeStruct((PANELS, BW...]
    all_gather x1 -> x0, waiting for transfers between devices: 47.4 us -> none  [device_fn(): pt = lax.all_gather(at[:bw], 'col', axis=0, tiled=True)]
    dot_general x5 -> x0, matrix products: 39.2 us -> none  [the longest x3 21.3 us: dot_nt(): lax.dot_general(x, y, (((1,), (1,)), ((), ())), precision=HIGHEST, prefer...]
    psum x1 -> x0, waiting for transfers between devices: 25.1 us -> none  [device_fn(): packed = lax.psum(jnp.concatenate([xt, head, gram, phead], axis=0), 'row')]
    slice x7 -> x0, local copies, waits for them, and re-layouts: 16.4 us -> none  [the longest x1 11.5 us: device_fn(): base = jnp.concatenate([jnp.zeros_like(at[:bw]), at[bw:]], axis=0)]
    all_gather x1 -> x0, local copies, waits for them, and re-layouts: 5.03 us -> none  [device_fn(): pt = lax.all_gather(at[:bw], 'col', axis=0, tiled=True)]
    another operation x1 -> x0, other arithmetic: 2.19 us -> none  [device_fn(): jnp.stack([tfull[j * bw:(j + 1) * bw, j * bw:(j + 1) * bw] for j in range...]
    ppermute x0 -> x3, starting transfers between devices: none -> 2.15 us  [device_fn(): lax.ppermute(xh, 'row', [(i, i ^ b) for i in range(4)])]
  transfers between devices with their start and end apart: 2 -> 3, of which waited for: 2 -> 0; matrix products, arithmetic and copies ran while one was open for 7% -> 0% of each run, Pallas kernels for 0% -> 19%
where the time goes in v2:
time: 117 us; the launch traced here: 116 us
  Pallas kernels  109 us (93%)
  local copies, waits for them, and re-layouts  4.6 us (4%)
  starting transfers between devices  2.15 us (2%)
    pallas_call x1, Pallas kernels, gather(): pl.pallas_call(gather_kernel, out_shape=(jax.ShapeDtypeStruct((PANELS, BW...  66.9 us
    pallas_call x1, Pallas kernels, factor(): pl.pallas_call(factor_kernel, out_shape=(sq, jax.ShapeDtypeStruct((PANELS...  22.6 us
    pallas_call x1, Pallas kernels, update(): pl.pallas_call(update_kernel, grid=(local_rows // lanes,), out_shape=jax....  19.3 us
    unnamed x12, local copies, waits for them, and re-layouts  4.6 us
  transfers between devices with their start and end apart: 3, of which 0 were waited for; matrix products, arithmetic and copies ran while one was open for 0% of the time, Pallas kernels for 19%

profile of v2, /device:TPU:0, one launch (start us, length us, event | category | flops | bytes accessed | tf_op | source)
XLA Modules:
  0.0 116.2 jit_solution(13024057704474927417)
XLA Ops:
  0.6 66.9 %gather.1 = (f32[4,32,4096]{2,1,0:T(8,128)S(1)}, f32[512,128]{1,0:T(8,128)S(1)}, f32[128,128]{1,0:T(8,128)S(1)}, f32[128,128]{1,0:T(8,128)S(1)}, f32[1024,128]{1,0:T(8,128)S(1)}) custom-call(f32[1024,4096]{1,0:T(8,128)} %bitcast.7), custom_call_target="tpu_custom_call" | custom-call | tf_op jit(solution)/shard_map/gather/pallas_call | solution.py:300
  67.5 0.0 copy-start.4
  67.5 0.6 copy-done.4
  68.1 0.0 copy-start.5
  68.1 0.6 copy-done.5
  68.8 0.7 collective-permute-start.2
  69.5 0.0 collective-permute-start.1
  69.5 1.5 %collective-permute-start = (f32[512,128]{1,0:T(8,128)S(1)}, f32[512,128]{1,0:T(8,128)}, u32[]{:S(2)}, u32[]{:S(2)}) collective-permute-start(f32[512,128]{1,0:T(8,128)S(1)} %get-tuple-element.15.x0_ref), channel_id=1, source_target_pairs={{0,2},{1,3},{2,0},{3,1},{4,6},{5,7},{6,4},{7,5},{8,10},{9,11},{10,... | collective-permute-start | bytes 786440 | tf_op jit(solution)/shard_map/ppermute | solution.py:399
  70.9 22.6 %factor.1 = (f32[128,128]{1,0:T(8,128)}, f32[4,32,32]{2,1,0:T(8,128)}, f32[1,128]{1,0:T(1,128)}, f32[128,128]{1,0:T(8,128)}, f32[128,128]{1,0:T(8,128)}, /*index=5*/f32[128,128]{1,0:T(8,128)}) custom-call(f32[128,128]{1,0:T(8,128)} %copy-done.4, f32[128,128]{1,0:T(8,128)} %copy-done.5), custom_call_target="tpu_custom_call" | custom-call | flops 400000000 | bytes 600000 | tf_op jit(solution)/shard_map/factor/pallas_call | solution.py:108
  93.5 0.0 collective-permute-done.2.x3_ref
  93.5 0.0 collective-permute-done.1.x2_ref
  93.5 0.0 collective-permute-done.x1_ref
  93.5 0.0 copy-start
  93.5 0.8 copy-done
  94.4 0.0 copy-start.1
  94.4 0.8 copy-done.1
  95.2 0.0 copy-start.2
  95.2 0.8 copy-done.2
  96.1 0.0 copy-start.3
  96.1 0.8 copy-done.3
  96.9 19.3 %update.1 = f32[1024,4096]{1,0:T(8,128)} custom-call(f32[1024,4096]{1,0:T(8,128)} %bitcast.8, f32[4,32,4096]{2,1,0:T(8,128)S(1)} %get-tuple-element.14.pt_ref, f32[512,128]{1,0:T(8,128)S(1)} %get-tuple-element.15.x0_ref, f32[512,128]{1,0:T(8,128)} %collective-permute-done.x1_ref, f32[512,128]{1,0:T(8,128)S(1)} %collective-permute-done.1.x2_ref, ...), custom_call_target="tpu_custom_call" | custom-call | tf_op jit(solution)/shard_map/update/pallas_call | solution.py:378
Async XLA Ops:
  67.5 0.6 copy-start.4
  68.1 0.6 copy-start.5
  68.8 24.8 %collective-permute-start.2 = (f32[512,128]{1,0:T(8,128)S(1)}, f32[512,128]{1,0:T(8,128)S(1)}, u32[]{:S(2)}, u32[]{:S(2)}) collective-permute-start(f32[512,128]{1,0:T(8,128)S(1)} %get-tuple-element.15.x0_ref), channel_id=1, source_target_pairs={{0,3},{1,2},{2,1},{3,0},{4,7},{5,6},{6,5},{7,4},{8,11},{9,10},{10,... | collective-permute-start | bytes 786440 | tf_op jit(solution)/shard_map/ppermute | solution.py:399
  69.5 24.1 %collective-permute-start.1 = (f32[512,128]{1,0:T(8,128)S(1)}, f32[512,128]{1,0:T(8,128)S(1)}, u32[]{:S(2)}, u32[]{:S(2)}) collective-permute-start(f32[512,128]{1,0:T(8,128)S(1)} %get-tuple-element.15.x0_ref), channel_id=1, source_target_pairs={{0,1},{1,0},{2,3},{3,2},{4,5},{5,4},{6,7},{7,6},{8,9},{9,8},{10,11... | collective-permute-start | bytes 786440 | tf_op jit(solution)/shard_map/ppermute | solution.py:399
  69.5 24.1 %collective-permute-start = (f32[512,128]{1,0:T(8,128)S(1)}, f32[512,128]{1,0:T(8,128)}, u32[]{:S(2)}, u32[]{:S(2)}) collective-permute-start(f32[512,128]{1,0:T(8,128)S(1)} %get-tuple-element.15.x0_ref), channel_id=1, source_target_pairs={{0,2},{1,3},{2,0},{3,1},{4,6},{5,7},{6,4},{7,5},{8,10},{9,11},{10,... | collective-permute-start | bytes 786440 | tf_op jit(solution)/shard_map/ppermute | solution.py:399
  93.5 0.8 copy-start
  94.4 0.8 copy-start.1
  95.2 0.8 copy-start.2
  96.1 0.8 copy-start.3

commit v3 on v2

--- a/solution.py
+++ b/solution.py
@@ -10,6 +10,9 @@
 BW = 32
 NC = PANELS * BW
 CH = 512
+UPDATE_VMEM = 32 * 1024 * 1024
+GATHER_VMEM = 32 * 1024 * 1024
+AHEAD = 3
 HIGHEST = lax.Precision.HIGHEST
 MESH = pl.DeviceIdType.MESH
 
@@ -111,14 +114,15 @@
         in_specs=[pl.BlockSpec(memory_space=pltpu.VMEM)] * 2,
         out_specs=tuple([pl.BlockSpec(memory_space=pltpu.VMEM)] * 6),
         scratch_shapes=[pltpu.VMEM((NC, NC), jnp.float32)] * 3,
+        compiler_params=pltpu.CompilerParams(vmem_limit_bytes=8 * 1024 * 1024),
         cost_estimate=pl.CostEstimate(flops=400_000_000, bytes_accessed=600_000, transcendentals=0),
         name="factor",
     )(gram, ptop)
 
 
-def gather_kernel(at_ref, pt_out, xh_out, g_out, ptop_out, head_out,
-                  a_v, pt_v, x_v, g_v, g_in, x_in, head_v, ptop_v,
-                  a_sem, own_sem, send_r, send_l, recv, h_sem, hsend, hrecv, psend, precv, gsend, grecv, xsend, xrecv, out_sem):
+def gather_kernel(at_ref, a_v, pt_out, xh_out, g_out, ptop_out, head_out,
+                  pt_v, x_v, g_v, g_in, x_in, head_v, ptop_v,
+                  a_sem, own_sem, send, fwd, recv, h_sem, hsend, hrecv, psend, precv, gsend, grecv, xsend, xrecv):
     ncol, local_rows = at_ref.shape
     nch = local_rows // CH
     half = ncol // 2
@@ -132,13 +136,19 @@
     def a_load(c):
         return pltpu.make_async_copy(at_ref.at[:, pl.ds(c * CH, CH)], a_v.at[c], a_sem.at[c])
 
-    def pt_store(c):
-        return pltpu.make_async_copy(pt_v.at[c], pt_out.at[:, :, pl.ds(c * CH, CH)], out_sem.at[c])
-
-    def hop(c, j, to, sems):
+    def hop(c, j, to, sem):
         return pltpu.make_async_remote_copy(
-            src_ref=pt_v.at[c, j], dst_ref=pt_v.at[c, j], send_sem=sems.at[c, j], recv_sem=recv.at[c, j],
+            src_ref=pt_v.at[c, j], dst_ref=pt_v.at[c, j], send_sem=sem, recv_sem=recv.at[c, j],
             device_id={'col': to}, device_id_type=MESH)
+
+    routes = ((q + 2, q + 2 <= last, 0), (q - 2, q >= 2, 1), (q + 1, q < last, 2), (q - 1, q > 0, 3))
+
+    def send_own(c):
+        own_load(c).wait()
+        for to, valid, slot in routes:
+            @pl.when(valid)
+            def _():
+                hop(c, q, to, send.at[c, slot]).start()
 
     def head_send(p):
         return pltpu.make_async_remote_copy(
@@ -157,13 +167,10 @@
 
     barrier = pltpu.get_barrier_semaphore()
 
-    @pl.when(q > 0)
-    def _():
-        pl.semaphore_signal(barrier, inc=1, device_id={'col': q - 1}, device_id_type=MESH)
-
-    @pl.when(q < last)
-    def _():
-        pl.semaphore_signal(barrier, inc=1, device_id={'col': q + 1}, device_id_type=MESH)
+    for to, valid, _ in routes:
+        @pl.when(valid)
+        def _():
+            pl.semaphore_signal(barrier, inc=1, device_id={'col': to}, device_id_type=MESH)
 
     for d in range(1, 4):
         pl.semaphore_signal(barrier, inc=1, device_id={'row': (r + d) % 4}, device_id_type=MESH)
@@ -171,22 +178,14 @@
 
     @pl.when(inner)
     def _():
+        pl.semaphore_wait(barrier, 6)
+
+    @pl.when(jnp.logical_not(inner))
+    def _():
         pl.semaphore_wait(barrier, 5)
 
-    @pl.when(jnp.logical_not(inner))
-    def _():
-        pl.semaphore_wait(barrier, 4)
-
-    for c in range(nch):
-        own_load(c).wait()
-
-        @pl.when(q < last)
-        def _():
-            hop(c, q, q + 1, send_r).start()
-
-        @pl.when(q > 0)
-        def _():
-            hop(c, q, q - 1, send_l).start()
+    for c in range(min(AHEAD, nch)):
+        send_own(c)
 
     head_local = pltpu.make_async_copy(at_ref.at[:, pl.ds(0, NC)], head_v, h_sem)
 
@@ -200,24 +199,29 @@
     g_v[...] = jnp.zeros_like(g_v)
 
     def chunk(c, carry):
+        @pl.when(c + AHEAD < nch)
+        def _():
+            send_own(c + AHEAD)
+
         for d in range(1, 4):
             @pl.when(q >= d)
             def _():
-                hop(c, q - d, q, send_r).wait_recv()
-
-                @pl.when(q < last)
-                def _():
-                    hop(c, q - d, q + 1, send_r).start()
+                hop(c, q - d, q, fwd.at[c]).wait_recv()
 
             @pl.when(q + d <= last)
             def _():
-                hop(c, q + d, q, send_l).wait_recv()
-
-                @pl.when(q > 0)
+                hop(c, q + d, q, fwd.at[c]).wait_recv()
+
+            if d == 2:
+                @pl.when(q == last - 1)
                 def _():
-                    hop(c, q + d, q - 1, send_l).start()
-
-        pt_store(c).start()
+                    hop(c, 0, q + 1, fwd.at[c]).start()
+
+                @pl.when(q == 1)
+                def _():
+                    hop(c, last, q - 1, fwd.at[c]).start()
+
+        pt_out[c] = pt_v[c]
 
         @pl.when(jnp.logical_and(c == 0, r == 0))
         def _():
@@ -261,19 +265,18 @@
         for j in range(PANELS):
             ptop_out[j * BW:(j + 1) * BW, :] = ptop_v[j]
 
-    head_store = pltpu.make_async_copy(head_v, head_out, h_sem)
-    head_store.start()
+    head_out[...] = head_v[...]
 
     def drain(c, carry):
-        pt_store(c).wait()
-        for j in range(PANELS):
-            @pl.when(jnp.logical_and(j <= q, q < last))
+        for to, valid, slot in routes:
+            @pl.when(valid)
             def _():
-                hop(c, j, q + 1, send_r).wait_send()
-
-            @pl.when(jnp.logical_and(j >= q, q > 0))
-            def _():
-                hop(c, j, q - 1, send_l).wait_send()
+                hop(c, q, to, send.at[c, slot]).wait_send()
+
+        @pl.when(inner)
+        def _():
+            hop(c, q, q, fwd.at[c]).wait_send()
+
         return carry
 
     lax.fori_loop(0, nch, drain, 0)
@@ -288,7 +291,6 @@
     g_out[...] = total
     x_copy.wait()
     xh_out[...] = x_v[pl.ds(half * core, half), :] + x_in[...]
-    head_store.wait()
 
 
 def gather(at):
@@ -299,16 +301,16 @@
     dma = pltpu.SemaphoreType.DMA
     return pl.pallas_call(
         gather_kernel,
-        out_shape=(jax.ShapeDtypeStruct((PANELS, BW, local_rows), f32), jax.ShapeDtypeStruct((ncol // 2, NC), f32),
+        out_shape=(jax.ShapeDtypeStruct((nch, ncol, CH), f32), jax.ShapeDtypeStruct((nch, PANELS, BW, CH), f32), jax.ShapeDtypeStruct((ncol // 2, NC), f32),
                    jax.ShapeDtypeStruct((NC, NC), f32), jax.ShapeDtypeStruct((NC, NC), f32), jax.ShapeDtypeStruct((ncol, NC), f32)),
         in_specs=[anys],
-        out_specs=(anys, vm, vm, vm, anys),
-        scratch_shapes=[pltpu.VMEM((nch, ncol, CH), f32), pltpu.VMEM((nch, PANELS, BW, CH), f32), pltpu.VMEM((ncol, NC), f32),
+        out_specs=(vm,) * 6,
+        scratch_shapes=[pltpu.VMEM((nch, PANELS, BW, CH), f32), pltpu.VMEM((ncol, NC), f32),
                         pltpu.VMEM((NC, NC), f32), pltpu.VMEM((3, NC, NC), f32), pltpu.VMEM((ncol // 2, NC), f32),
                         pltpu.VMEM((ncol, NC), f32), pltpu.VMEM((PANELS, BW, NC), f32),
-                        dma((nch,)), dma((nch,)), dma((nch, 4)), dma((nch, 4)), dma((nch, 4)), dma, dma((4,)), dma, dma((4,)), dma,
-                        dma((3,)), dma((3,)), dma, dma, dma((nch,))],
-        compiler_params=pltpu.CompilerParams(collective_id=0, has_side_effects=True, vmem_limit_bytes=48 * 1024 * 1024),
+                        dma((nch,)), dma((nch,)), dma((nch, 4)), dma((nch,)), dma((nch, 4)), dma, dma((4,)), dma, dma((4,)), dma,
+                        dma((3,)), dma((3,)), dma, dma],
+        compiler_params=pltpu.CompilerParams(collective_id=0, has_side_effects=True, vmem_limit_bytes=GATHER_VMEM),
         name="gather",
     )(at)
 
@@ -321,7 +323,13 @@
     return hi, mid, lo
 
 
-def update_kernel(at_ref, pt_ref, x0_ref, x1_ref, x2_ref, x3_ref, head_ref, rit_ref, nmat_ref, uit_ref, facet_ref, out_ref, zhm_v, zhl_v, top_v):
+def store_split(dst, rows, z):
+    zh, zm, zl = split3(z)
+    for i, part in enumerate((zh, zm, zh, zm, zh, zl)):
+        dst[rows, i * NC:(i + 1) * NC] = part
+
+
+def update_kernel(a_ref, pt_ref, x0_ref, x1_ref, x2_ref, x3_ref, head_ref, rit_ref, nmat_ref, uit_ref, facet_ref, out_ref, z_v, top_v):
     step = pl.program_id(0)
     q = lax.axis_index('col')
     r = lax.axis_index('row')
@@ -338,31 +346,15 @@
         for lo, xa, xb in ((mine, x0_ref, x1_ref), (other, x2_ref, x3_ref)):
             r12t = dot_nt(xa[...] + xb[...], rit)
             top_v[pl.ds(lo, half), :] = r12t
-            z = dot_nn(head_ref[pl.ds(lo, half), :] - r12t, nmat)
-            zh, zm, zl = split3(z)
-            zhm_v[pl.ds(lo, half), 0:NC] = zh
-            zhm_v[pl.ds(lo, half), NC:2 * NC] = zm
-            zhl_v[pl.ds(lo, half), 0:NC] = zh
-            zhl_v[pl.ds(lo, half), NC:2 * NC] = zl
+            store_split(z_v, pl.ds(lo, half), dot_nn(head_ref[pl.ds(lo, half), :] - r12t, nmat))
         own = pl.ds(pl.multiple_of(q * BW, BW), BW)
         top_v[0:BW, :] = facet_ref[own, :]
-        zh, zm, zl = split3(-uit_ref[own, :])
-        zhm_v[0:BW, 0:NC] = zh
-        zhm_v[0:BW, NC:2 * NC] = zm
-        zhl_v[0:BW, 0:NC] = zh
-        zhl_v[0:BW, NC:2 * NC] = zl
-
-    ph, pm, plo = split3(pt_ref[...].reshape(NC, pt_ref.shape[2]))
-    w_hm = jnp.concatenate([ph, pm], axis=0)
-    w_mh = jnp.concatenate([pm, ph], axis=0)
-    w_lh = jnp.concatenate([plo, ph], axis=0)
-
-    def dot16(x, y):
-        return lax.dot_general(x, y, (((1,), (0,)), ((), ())), preferred_element_type=jnp.float32)
-
-    zhm = zhm_v[...]
-    prod = dot16(zhm, w_hm) + (dot16(zhm, w_mh) + dot16(zhl_v[...], w_lh))
-    out_ref[BW:, :] = at_ref[BW:, :] - prod[BW:]
+        store_split(z_v, pl.ds(0, BW), -uit_ref[own, :])
+
+    ph, pm, plo = split3(pt_ref[step].reshape(NC, CH))
+    wide = jnp.concatenate([ph, pm, pm, ph, plo, ph], axis=0)
+    prod = lax.dot_general(z_v[...], wide, (((1,), (0,)), ((), ())), preferred_element_type=jnp.float32)
+    out_ref[BW:, :] = a_ref[step, BW:, :] - prod[BW:]
     out_ref[0:BW, :] = -prod[0:BW]
 
     @pl.when(jnp.logical_and(step == 0, r == 0))
@@ -370,22 +362,19 @@
         out_ref[:, 0:NC] = top_v[...]
 
 
-def update(at, pt, xs, head, rit, nmat, uit, facet):
-    ncol, local_rows = at.shape
-    lanes = 512
-    full = lambda a: pl.BlockSpec(a.shape, lambda i: (0,) * a.ndim)
-    strip = pl.BlockSpec((ncol, lanes), lambda i: (0, i))
+def update(a, pt, xs, head, rit, nmat, uit, facet):
+    nch, ncol, _ = a.shape
+    vm = pl.BlockSpec(memory_space=pltpu.VMEM)
     return pl.pallas_call(
         update_kernel,
-        grid=(local_rows // lanes,),
-        out_shape=jax.ShapeDtypeStruct(at.shape, jnp.float32),
-        in_specs=[strip, pl.BlockSpec((PANELS, BW, lanes), lambda i: (0, 0, i))] + [full(x) for x in xs]
-        + [full(head), full(rit), full(nmat), full(uit), full(facet)],
-        out_specs=strip,
-        scratch_shapes=[pltpu.VMEM((ncol, 2 * NC), jnp.bfloat16), pltpu.VMEM((ncol, 2 * NC), jnp.bfloat16), pltpu.VMEM((ncol, NC), jnp.float32)],
-        compiler_params=pltpu.CompilerParams(dimension_semantics=("arbitrary",), vmem_limit_bytes=48 * 1024 * 1024),
+        grid=(nch,),
+        out_shape=jax.ShapeDtypeStruct((ncol, nch * CH), jnp.float32),
+        in_specs=[vm] * 11,
+        out_specs=pl.BlockSpec((ncol, CH), lambda i: (0, i)),
+        scratch_shapes=[pltpu.VMEM((ncol, 6 * NC), jnp.bfloat16), pltpu.VMEM((ncol, NC), jnp.float32)],
+        compiler_params=pltpu.CompilerParams(dimension_semantics=("arbitrary",), vmem_limit_bytes=UPDATE_VMEM),
         name="update",
-    )(at, pt, *xs, head, rit, nmat, uit, facet)
+    )(a, pt, *xs, head, rit, nmat, uit, facet)
 
 
 def solution(mesh):
@@ -395,10 +384,10 @@
         local_rows, local_blocks, bw = a_local.shape
         ncol = local_blocks * bw
         at = a_local.transpose(1, 2, 0).reshape(ncol, local_rows)
-        pt, xh, gram, ptop, head = gather(at)
+        a, pt, xh, gram, ptop, head = gather(at)
         x1, x2, x3 = [lax.ppermute(xh, 'row', [(i, i ^ b) for i in range(4)]) for b in (2, 1, 3)]
         facet, tfac, tau, rit, nmat, uit = factor(gram, ptop)
-        out = update(at, pt, (xh, x1, x2, x3), head, rit, nmat, uit, facet)
+        out = update(a, pt, (xh, x1, x2, x3), head, rit, nmat, uit, facet)
         a_out = out.reshape(local_blocks, bw, local_rows).transpose(2, 0, 1)
         return a_out, tau.reshape(NC), tfac
 

time: 117 us -> 88 us (0.75)
  Pallas kernels: 109 us -> 84.9 us
  local copies, waits for them, and re-layouts: 4.6 us -> 0 us
    pallas_call x2, Pallas kernels: 86.2 us -> 63.2 us  [the longest x1 50.9 us: gather(): pl.pallas_call(gather_kernel, out_shape=(jax.ShapeDtypeStruct((nch, ncol,...]
    unnamed x12 -> x0, local copies, waits for them, and re-layouts: 4.6 us -> none
  transfers between devices with their start and end apart: 3 -> 3, of which waited for: 0 -> 0; matrix products, arithmetic and copies ran while one was open for 0% -> 0% of each run, Pallas kernels for 19% -> 25%
where the time goes in v3:
time: 88 us; the launch traced here: 87.8 us
  Pallas kernels  84.9 us (96%)
  starting transfers between devices  2.22 us (3%)
    pallas_call x1, Pallas kernels, gather(): pl.pallas_call(gather_kernel, out_shape=(jax.ShapeDtypeStruct((nch, ncol,...  50.9 us
    pallas_call x1, Pallas kernels, factor(): pl.pallas_call(factor_kernel, out_shape=(sq, jax.ShapeDtypeStruct((PANELS...  21.7 us
    pallas_call x1, Pallas kernels, update(): pl.pallas_call(update_kernel, grid=(nch,), out_shape=jax.ShapeDtypeStruct...  12.3 us
    ppermute x3, starting transfers between devices, device_fn(): lax.ppermute(xh, 'row', [(i, i ^ b) for i in range(4)])  2.22 us
  transfers between devices with their start and end apart: 3, of which 0 were waited for; matrix products, arithmetic and copies ran while one was open for 0% of the time, Pallas kernels for 25%

profile of v3, /device:TPU:0, one launch (start us, length us, event | category | flops | bytes accessed | tf_op | source)
XLA Modules:
  0.0 87.8 jit_solution(16232255081484758236)
XLA Ops:
  0.6 50.9 %gather.1 = (f32[8,1024,512]{2,1,0:T(8,128)S(1)}, f32[8,4,32,512]{3,2,1,0:T(8,128)S(1)}, f32[512,128]{1,0:T(8,128)S(1)}, f32[128,128]{1,0:T(8,128)S(1)}, f32[128...) custom-call(f32[1024,4096]{1,0:T(8,128)} %bitcast.7), custom_call_target="tpu_custom_call" | custom-call | tf_op jit(solution)/shard_map/gather/pallas_call | solution.py:302
  51.6 0.7 collective-permute-start.2
  52.3 0.0 collective-permute-start.1
  52.3 1.5 %collective-permute-start = (f32[512,128]{1,0:T(8,128)S(1)}, f32[512,128]{1,0:T(8,128)S(1)}, u32[]{:S(2)}, u32[]{:S(2)}) collective-permute-start(f32[512,128]{1,0:T(8,128)S(1)} %get-tuple-element.17.x0_ref), channel_id=1, source_target_pairs={{0,2},{1,3},{2,0},{3,1},{4,6},{5,7},{6,4},{7,5},{8,10},{9,11},{10,... | collective-permute-start | bytes 786440 | tf_op jit(solution)/shard_map/ppermute | solution.py:388
  53.8 21.7 %factor.1 = (f32[128,128]{1,0:T(8,128)S(1)}, f32[4,32,32]{2,1,0:T(8,128)}, f32[1,128]{1,0:T(1,128)}, f32[128,128]{1,0:T(8,128)S(1)}, f32[128,128]{1,0:T(8,128)S(1)}, /*index=5*/f32[128,128]{1,0:T(8,128)S(1)}) custom-call(f32[128,128]{1,0:T(8,128)S(1)} %get-tuple-element.19.g_ref, f32[128,128]{1,0:T(8,128)S(1)} %get-tuple-element.20.ptop_ref), custom_call_target="tpu_custom_call" | custom-call | flops 400000000 | bytes 600000 | tf_op jit(solution)/shard_map/factor/pallas_call | solution.py:111
  75.5 0.0 collective-permute-done.2.x3_ref
  75.5 0.0 collective-permute-done.1.x2_ref
  75.5 0.0 collective-permute-done.x1_ref
  75.5 12.3 %update.1 = f32[1024,4096]{1,0:T(8,128)} custom-call(f32[8,1024,512]{2,1,0:T(8,128)S(1)} %get-tuple-element.15.a_ref, f32[8,4,32,512]{3,2,1,0:T(8,128)S(1)} %get-tuple-element.16.pt_ref, f32[512,128]{1,0:T(8,128)S(1)} %get-tuple-element.17.x0_ref, f32[512,128]{1,0:T(8,128)S(1)} %collective-permute-done.x1_ref, f32[512,128]{1,0:T(8,128)S(1)} %collective-permute-done.1.x2_ref, ...), custom_call_target="tpu_custom_call" | custom-call | tf_op jit(solution)/shard_map/update/pallas_call | solution.py:368
Async XLA Ops:
  51.6 24.0 %collective-permute-start.2 = (f32[512,128]{1,0:T(8,128)S(1)}, f32[512,128]{1,0:T(8,128)S(1)}, u32[]{:S(2)}, u32[]{:S(2)}) collective-permute-start(f32[512,128]{1,0:T(8,128)S(1)} %get-tuple-element.17.x0_ref), channel_id=1, source_target_pairs={{0,3},{1,2},{2,1},{3,0},{4,7},{5,6},{6,5},{7,4},{8,11},{9,10},{10,... | collective-permute-start | bytes 786440 | tf_op jit(solution)/shard_map/ppermute | solution.py:388
  52.3 23.3 %collective-permute-start.1 = (f32[512,128]{1,0:T(8,128)S(1)}, f32[512,128]{1,0:T(8,128)S(1)}, u32[]{:S(2)}, u32[]{:S(2)}) collective-permute-start(f32[512,128]{1,0:T(8,128)S(1)} %get-tuple-element.17.x0_ref), channel_id=1, source_target_pairs={{0,1},{1,0},{2,3},{3,2},{4,5},{5,4},{6,7},{7,6},{8,9},{9,8},{10,11... | collective-permute-start | bytes 786440 | tf_op jit(solution)/shard_map/ppermute | solution.py:388
  52.3 23.3 %collective-permute-start = (f32[512,128]{1,0:T(8,128)S(1)}, f32[512,128]{1,0:T(8,128)S(1)}, u32[]{:S(2)}, u32[]{:S(2)}) collective-permute-start(f32[512,128]{1,0:T(8,128)S(1)} %get-tuple-element.17.x0_ref), channel_id=1, source_target_pairs={{0,2},{1,3},{2,0},{3,1},{4,6},{5,7},{6,4},{7,5},{8,10},{9,11},{10,... | collective-permute-start | bytes 786440 | tf_op jit(solution)/shard_map/ppermute | solution.py:388

commit v4 on v3

--- a/solution.py
+++ b/solution.py
@@ -48,41 +48,73 @@
     inv_row = jnp.zeros((8, NC), jnp.float32)
     tau_row = jnp.zeros((8, NC), jnp.float32)
     invs = []
-    for k in range(NC):
-        t0, s = divmod(k, 8)
-        gcol = [col_of(g[t], k) for t in range(t0, nt)]
-        bcol = [col_of(b[t], k) for t in range(t0, nt)]
-        diag = row_of(gcol[0], s)
-        rs = lax.rsqrt(diag)
-        rrow = jnp.where(lane >= k, row_of(g[t0], s) * rs, 0.0)
-        rirow = row_of(ri[t0], s) * rs
-        for t in range(t0, nt):
-            f = gcol[t - t0] * rs
-            g[t] = g[t] - f * rrow
-            ri[t] = ri[t] - f * rirow
-        norm = diag * rs
-        alpha = row_of(bcol[0], s)
-        sgn = jnp.where(alpha >= 0.0, 1.0, -1.0)
-        beta = -sgn * norm
-        rsig = -sgn * rrow
-        brow = row_of(b[t0], s)
-        urow = jnp.where(lane >= k, brow - rsig, 0.0)
-        piv = alpha - beta
-        inv = 1.0 / piv
-        tau_row = jnp.where(lane == k, (beta - alpha) / beta, tau_row)
-        lrow = brow * inv_row
-        inv_row = jnp.where(lane == k, inv, inv_row)
-        uupd = jnp.where(lane > k, urow, 0.0)
-        lirow = row_of(li[t0], s)
-        for t in range(t0, nt):
-            f = bcol[t - t0] * inv
-            b[t] = b[t] - f * uupd
-            li[t] = li[t] - f * lirow
-        face_ref[k:k + 1, :] = jnp.where(lane >= k, rsig, lrow)[0:1]
-        u_ref[k:k + 1, :] = urow[0:1]
-        rit_ref[k:k + 1, :] = (-sgn * rirow)[0:1]
-        li_ref[k:k + 1, :] = lirow[0:1]
-        invs.append(inv)
+
+    def trail(t, block, steps, width):
+        for lo in range(0, 8, width):
+            cg = {s: col_of(g[t], 8 * block + s) for s in range(lo, lo + width)}
+            cb = {s: col_of(b[t], 8 * block + s) for s in range(lo, lo + width)}
+            for s in range(lo, lo + width):
+                rs, inv, rrow, rirow, uupd, lirow, rj, uj = steps[s]
+                fg = cg[s] * rs
+                fb = cb[s] * inv
+                g[t] = g[t] - fg * rrow
+                ri[t] = ri[t] - fg * rirow
+                b[t] = b[t] - fb * uupd
+                li[t] = li[t] - fb * lirow
+                for j in range(s + 1, lo + width):
+                    cg[j] = cg[j] - fg * rj[j]
+                    cb[j] = cb[j] - fb * uj[j]
+
+    pending = []
+    for block in range(nt):
+        gd, bd, rid, lid = g[block], b[block], ri[block], li[block]
+        cg = [col_of(gd, 8 * block + s) for s in range(8)]
+        cb = [col_of(bd, 8 * block + s) for s in range(8)]
+        steps = []
+        share = -(-len(pending) // 8)
+        for s in range(8):
+            k = 8 * block + s
+            diag = row_of(cg[s], s)
+            rs = lax.rsqrt(diag)
+            norm = diag * rs
+            alpha = row_of(cb[s], s)
+            sgn = jnp.where(alpha >= 0.0, 1.0, -1.0)
+            beta = -sgn * norm
+            inv = 1.0 / (alpha - beta)
+            fg = cg[s] * rs
+            fb = cb[s] * inv
+            rj, uj = {}, {}
+            for j in range(s + 1, 8):
+                rj[j] = row_of(fg, j)
+                uj[j] = row_of(cb[j], s) + sgn * rj[j]
+                cg[j] = cg[j] - fg * rj[j]
+                cb[j] = cb[j] - fb * uj[j]
+            rrow = jnp.where(lane >= k, row_of(gd, s) * rs, 0.0)
+            rirow = row_of(rid, s) * rs
+            lirow = row_of(lid, s)
+            brow = row_of(bd, s)
+            rsig = -sgn * rrow
+            urow = jnp.where(lane >= k, brow - rsig, 0.0)
+            uupd = jnp.where(lane > k, urow, 0.0)
+            gd = gd - fg * rrow
+            rid = rid - fg * rirow
+            bd = bd - fb * uupd
+            lid = lid - fb * lirow
+            steps.append((rs, inv, rrow, rirow, uupd, lirow, rj, uj))
+            tau_row = jnp.where(lane == k, (beta - alpha) / beta, tau_row)
+            lrow = brow * inv_row
+            inv_row = jnp.where(lane == k, inv, inv_row)
+            face_ref[k:k + 1, :] = jnp.where(lane >= k, rsig, lrow)[0:1]
+            u_ref[k:k + 1, :] = urow[0:1]
+            rit_ref[k:k + 1, :] = (-sgn * rirow)[0:1]
+            li_ref[k:k + 1, :] = lirow[0:1]
+            invs.append(inv)
+            for args in pending[:share]:
+                trail(*args)
+            pending = pending[share:]
+        if block + 1 < nt:
+            trail(block + 1, block, steps, 8)
+        pending = [(t, block, steps, 4) for t in range(block + 2, nt)]
     tau_ref[...] = tau_row[0:1]
     facet_ref[...] = face_ref[...].T
     umat = u_ref[...]

time: 88 us -> 83.9 us (0.953)
  Pallas kernels: 84.9 us -> 80.9 us
    pallas_call x1, Pallas kernels: 21.7 us -> 17.6 us  [factor(): pl.pallas_call(factor_kernel, out_shape=(sq, jax.ShapeDtypeStruct((PANELS...]
  transfers between devices with their start and end apart: 3 -> 3, of which waited for: 0 -> 0; matrix products, arithmetic and copies ran while one was open for 0% -> 0% of each run, Pallas kernels for 25% -> 21%
where the time goes in v4:
time: 83.9 us; the launch traced here: 83.7 us
  Pallas kernels  80.9 us (96%)
  starting transfers between devices  2.22 us (3%)
    pallas_call x1, Pallas kernels, gather(): pl.pallas_call(gather_kernel, out_shape=(jax.ShapeDtypeStruct((nch, ncol,...  50.9 us
    pallas_call x1, Pallas kernels, factor(): pl.pallas_call(factor_kernel, out_shape=(sq, jax.ShapeDtypeStruct((PANELS...  17.6 us
    pallas_call x1, Pallas kernels, update(): pl.pallas_call(update_kernel, grid=(nch,), out_shape=jax.ShapeDtypeStruct...  12.3 us
    ppermute x3, starting transfers between devices, device_fn(): lax.ppermute(xh, 'row', [(i, i ^ b) for i in range(4)])  2.22 us
  transfers between devices with their start and end apart: 3, of which 0 were waited for; matrix products, arithmetic and copies ran while one was open for 0% of the time, Pallas kernels for 21%

profile of v4, /device:TPU:0, one launch (start us, length us, event | category | flops | bytes accessed | tf_op | source)
XLA Modules:
  0.0 83.7 jit_solution(9456927958192738721)
XLA Ops:
  0.6 50.9 %gather.1 = (f32[8,1024,512]{2,1,0:T(8,128)S(1)}, f32[8,4,32,512]{3,2,1,0:T(8,128)S(1)}, f32[512,128]{1,0:T(8,128)S(1)}, f32[128,128]{1,0:T(8,128)S(1)}, f32[128...) custom-call(f32[1024,4096]{1,0:T(8,128)} %bitcast.7), custom_call_target="tpu_custom_call" | custom-call | tf_op jit(solution)/shard_map/gather/pallas_call | solution.py:334
  51.6 0.7 collective-permute-start.2
  52.3 0.0 collective-permute-start.1
  52.3 1.5 %collective-permute-start = (f32[512,128]{1,0:T(8,128)S(1)}, f32[512,128]{1,0:T(8,128)S(1)}, u32[]{:S(2)}, u32[]{:S(2)}) collective-permute-start(f32[512,128]{1,0:T(8,128)S(1)} %get-tuple-element.17.x0_ref), channel_id=1, source_target_pairs={{0,2},{1,3},{2,0},{3,1},{4,6},{5,7},{6,4},{7,5},{8,10},{9,11},{10,... | collective-permute-start | bytes 786440 | tf_op jit(solution)/shard_map/ppermute | solution.py:420
  53.8 17.6 %factor.1 = (f32[128,128]{1,0:T(8,128)S(1)}, f32[4,32,32]{2,1,0:T(8,128)}, f32[1,128]{1,0:T(1,128)}, f32[128,128]{1,0:T(8,128)S(1)}, f32[128,128]{1,0:T(8,128)S(1)}, /*index=5*/f32[128,128]{1,0:T(8,128)S(1)}) custom-call(f32[128,128]{1,0:T(8,128)S(1)} %get-tuple-element.19.g_ref, f32[128,128]{1,0:T(8,128)S(1)} %get-tuple-element.20.ptop_ref), custom_call_target="tpu_custom_call" | custom-call | flops 400000000 | bytes 600000 | tf_op jit(solution)/shard_map/factor/pallas_call | solution.py:143
  71.4 0.0 collective-permute-done.2.x3_ref
  71.4 0.0 collective-permute-done.1.x2_ref
  71.4 0.0 collective-permute-done.x1_ref
  71.4 12.3 %update.1 = f32[1024,4096]{1,0:T(8,128)} custom-call(f32[8,1024,512]{2,1,0:T(8,128)S(1)} %get-tuple-element.15.a_ref, f32[8,4,32,512]{3,2,1,0:T(8,128)S(1)} %get-tuple-element.16.pt_ref, f32[512,128]{1,0:T(8,128)S(1)} %get-tuple-element.17.x0_ref, f32[512,128]{1,0:T(8,128)S(1)} %collective-permute-done.x1_ref, f32[512,128]{1,0:T(8,128)S(1)} %collective-permute-done.1.x2_ref, ...), custom_call_target="tpu_custom_call" | custom-call | tf_op jit(solution)/shard_map/update/pallas_call | solution.py:400
Async XLA Ops:
  51.6 19.9 %collective-permute-start.2 = (f32[512,128]{1,0:T(8,128)S(1)}, f32[512,128]{1,0:T(8,128)S(1)}, u32[]{:S(2)}, u32[]{:S(2)}) collective-permute-start(f32[512,128]{1,0:T(8,128)S(1)} %get-tuple-element.17.x0_ref), channel_id=1, source_target_pairs={{0,3},{1,2},{2,1},{3,0},{4,7},{5,6},{6,5},{7,4},{8,11},{9,10},{10,... | collective-permute-start | bytes 786440 | tf_op jit(solution)/shard_map/ppermute | solution.py:420
  52.3 19.2 %collective-permute-start.1 = (f32[512,128]{1,0:T(8,128)S(1)}, f32[512,128]{1,0:T(8,128)S(1)}, u32[]{:S(2)}, u32[]{:S(2)}) collective-permute-start(f32[512,128]{1,0:T(8,128)S(1)} %get-tuple-element.17.x0_ref), channel_id=1, source_target_pairs={{0,1},{1,0},{2,3},{3,2},{4,5},{5,4},{6,7},{7,6},{8,9},{9,8},{10,11... | collective-permute-start | bytes 786440 | tf_op jit(solution)/shard_map/ppermute | solution.py:420
  52.3 19.2 %collective-permute-start = (f32[512,128]{1,0:T(8,128)S(1)}, f32[512,128]{1,0:T(8,128)S(1)}, u32[]{:S(2)}, u32[]{:S(2)}) collective-permute-start(f32[512,128]{1,0:T(8,128)S(1)} %get-tuple-element.17.x0_ref), channel_id=1, source_target_pairs={{0,2},{1,3},{2,0},{3,1},{4,6},{5,7},{6,4},{7,5},{8,10},{9,11},{10,... | collective-permute-start | bytes 786440 | tf_op jit(solution)/shard_map/ppermute | solution.py:420

commit v5 on v4

--- a/solution.py
+++ b/solution.py
@@ -29,10 +29,29 @@
     return lax.dot_general(x, y, (((0,), (0,)), ((), ())), precision=HIGHEST, preferred_element_type=jnp.float32)
 
 
-def factor_kernel(g_ref, ptop_ref, facet_ref, tfac_ref, tau_ref, rit_ref, nmat_ref, uit_ref, u_ref, li_ref, face_ref):
+def split3(x):
+    hi = x.astype(jnp.bfloat16)
+    rem = x - hi.astype(jnp.float32)
+    mid = rem.astype(jnp.bfloat16)
+    lo = (rem - mid.astype(jnp.float32)).astype(jnp.bfloat16)
+    return hi, mid, lo
+
+
+def outer48(x, y):
+    xh, xm, xl = [p.astype(jnp.float32) for p in split3(x)]
+    yh, ym, yl = [p.astype(jnp.float32) for p in split3(y)]
+    left = jnp.concatenate([xh, xm, xh, xm, xh, xl], axis=0).astype(jnp.bfloat16)
+    right = jnp.concatenate([yh, ym, ym, yh, yl, yh], axis=0).astype(jnp.bfloat16)
+    return lax.dot_general(left, right, (((0,), (0,)), ((), ())), preferred_element_type=jnp.float32)
+
+
+def factor_kernel(g_ref, ptop_ref, facet_ref, tau_ref, tau8_ref, rit_ref, uit_ref, u_ref, li_ref, gr_v, bl_v, te_v, r_v, lt_v):
     nt = NC // 8
     lane = lax.broadcasted_iota(jnp.int32, (8, NC), 1)
     sub = lax.broadcasted_iota(jnp.int32, (8, NC), 0)
+    rows = lax.broadcasted_iota(jnp.int32, (NC, NC), 0)
+    cols = lax.broadcasted_iota(jnp.int32, (NC, NC), 1)
+    eye = jnp.where(rows == cols, 1.0, 0.0)
 
     def row_of(tile, s):
         return jnp.broadcast_to(tile[s:s + 1, :], (8, NC))
@@ -40,40 +59,25 @@
     def col_of(tile, k):
         return jnp.broadcast_to(tile[:, k:k + 1], (8, NC))
 
-    g = [g_ref[8 * t:8 * t + 8, :] for t in range(nt)]
-    top = ptop_ref[...].T
-    b = [top[8 * t:8 * t + 8, :] for t in range(nt)]
-    ri = [jnp.where(lane == sub + 8 * t, 1.0, 0.0) for t in range(nt)]
-    li = [jnp.where(lane == sub + 8 * t, 1.0, 0.0) for t in range(nt)]
-    inv_row = jnp.zeros((8, NC), jnp.float32)
+    gr_v[:, 0:NC] = g_ref[...]
+    bl_v[:, 0:NC] = ptop_ref[...].T
+    te_v[:, 0:NC] = ptop_ref[...]
+    for ref in (gr_v, bl_v, te_v):
+        ref[:, NC:2 * NC] = eye
     tau_row = jnp.zeros((8, NC), jnp.float32)
-    invs = []
-
-    def trail(t, block, steps, width):
-        for lo in range(0, 8, width):
-            cg = {s: col_of(g[t], 8 * block + s) for s in range(lo, lo + width)}
-            cb = {s: col_of(b[t], 8 * block + s) for s in range(lo, lo + width)}
-            for s in range(lo, lo + width):
-                rs, inv, rrow, rirow, uupd, lirow, rj, uj = steps[s]
-                fg = cg[s] * rs
-                fb = cb[s] * inv
-                g[t] = g[t] - fg * rrow
-                ri[t] = ri[t] - fg * rirow
-                b[t] = b[t] - fb * uupd
-                li[t] = li[t] - fb * lirow
-                for j in range(s + 1, lo + width):
-                    cg[j] = cg[j] - fg * rj[j]
-                    cb[j] = cb[j] - fb * uj[j]
-
-    pending = []
+    gr, bl, te = gr_v[0:8, :], bl_v[0:8, :], te_v[0:8, :]
     for block in range(nt):
-        gd, bd, rid, lid = g[block], b[block], ri[block], li[block]
-        cg = [col_of(gd, 8 * block + s) for s in range(8)]
-        cb = [col_of(bd, 8 * block + s) for s in range(8)]
-        steps = []
-        share = -(-len(pending) // 8)
+        o = 8 * block
+        gd, rid = gr[:, 0:NC], gr[:, NC:]
+        bd, lid = bl[:, 0:NC], bl[:, NC:]
+        cg = [col_of(gd, o + s) for s in range(8)]
+        cb = [col_of(bd, o + s) for s in range(8)]
+        bt = [row_of(te[:, 0:NC], s) for s in range(8)]
+        e = [row_of(te[:, NC:], s) for s in range(8)]
+        zero = jnp.zeros((8, NC), jnp.float32)
+        r_b = ri_b = u_b = li_b = l_b = y_b = neg = zero
         for s in range(8):
-            k = 8 * block + s
+            k = o + s
             diag = row_of(cg[s], s)
             rs = lax.rsqrt(diag)
             norm = diag * rs
@@ -83,73 +87,91 @@
             inv = 1.0 / (alpha - beta)
             fg = cg[s] * rs
             fb = cb[s] * inv
-            rj, uj = {}, {}
+            lrow = jnp.where(lane > k, bt[s] * inv, 0.0)
+            yrow = e[s] * inv
             for j in range(s + 1, 8):
-                rj[j] = row_of(fg, j)
-                uj[j] = row_of(cb[j], s) + sgn * rj[j]
-                cg[j] = cg[j] - fg * rj[j]
-                cb[j] = cb[j] - fb * uj[j]
+                rj = row_of(fg, j)
+                uj = row_of(cb[j], s) + sgn * rj
+                cg[j] = cg[j] - fg * rj
+                cb[j] = cb[j] - fb * uj
+                bt[j] = bt[j] - lrow * uj
+                e[j] = e[j] - yrow * uj
             rrow = jnp.where(lane >= k, row_of(gd, s) * rs, 0.0)
             rirow = row_of(rid, s) * rs
             lirow = row_of(lid, s)
-            brow = row_of(bd, s)
-            rsig = -sgn * rrow
-            urow = jnp.where(lane >= k, brow - rsig, 0.0)
-            uupd = jnp.where(lane > k, urow, 0.0)
+            urow = jnp.where(lane >= k, row_of(bd, s) + sgn * rrow, 0.0)
             gd = gd - fg * rrow
             rid = rid - fg * rirow
-            bd = bd - fb * uupd
+            bd = bd - fb * urow
             lid = lid - fb * lirow
-            steps.append((rs, inv, rrow, rirow, uupd, lirow, rj, uj))
+            here = sub == s
+            r_b = jnp.where(here, rrow, r_b)
+            ri_b = jnp.where(here, rirow, ri_b)
+            u_b = jnp.where(here, urow, u_b)
+            li_b = jnp.where(here, lirow, li_b)
+            l_b = jnp.where(here, lrow, l_b)
+            y_b = jnp.where(here, yrow, y_b)
+            neg = jnp.where(here, -sgn, neg)
             tau_row = jnp.where(lane == k, (beta - alpha) / beta, tau_row)
-            lrow = brow * inv_row
-            inv_row = jnp.where(lane == k, inv, inv_row)
-            face_ref[k:k + 1, :] = jnp.where(lane >= k, rsig, lrow)[0:1]
-            u_ref[k:k + 1, :] = urow[0:1]
-            rit_ref[k:k + 1, :] = (-sgn * rirow)[0:1]
-            li_ref[k:k + 1, :] = lirow[0:1]
-            invs.append(inv)
-            for args in pending[:share]:
-                trail(*args)
-            pending = pending[share:]
+        tile = slice(o, o + 8)
+        r_v[tile, :] = r_b * neg
+        rit_ref[tile, :] = ri_b * neg
+        u_ref[tile, :] = u_b
+        li_ref[tile, :] = li_b
+        lt_v[tile, :] = l_b
+        uit_ref[tile, :] = y_b
         if block + 1 < nt:
-            trail(block + 1, block, steps, 8)
-        pending = [(t, block, steps, 4) for t in range(block + 2, nt)]
+            new = []
+            for ref, x, y in ((gr_v, r_b, (r_b, ri_b)), (bl_v, l_b, (u_b, li_b)), (te_v, u_b, (l_b, y_b))):
+                prod = outer48(x, jnp.concatenate(y, axis=1))
+                new.append(ref[o + 8:o + 16, :] - prod[o + 8:o + 16])
+                if block + 2 < nt:
+                    ref[o + 16:, :] = ref[o + 16:, :] - prod[o + 16:]
+            gr, bl, te = new
     tau_ref[...] = tau_row[0:1]
-    facet_ref[...] = face_ref[...].T
-    umat = u_ref[...]
-    ut = umat.T
-    u_t = [ut[8 * t:8 * t + 8, :] for t in range(nt)]
-    e = [jnp.where(lane == sub + 8 * t, 1.0, 0.0) for t in range(nt)]
-    for k in range(NC):
-        t0, s = divmod(k, 8)
-        yrow = row_of(e[t0], s) * invs[k]
-        uit_ref[k:k + 1, :] = yrow[0:1]
-        for t in range(t0, nt):
-            e[t] = e[t] - col_of(u_t[t], k) * yrow
+    tau8_ref[...] = tau_row
+    facet_ref[...] = jnp.where(cols > rows, lt_v[...], r_v[...].T)
+
+
+def finish_kernel(tau8_ref, rit_ref, uit_ref, u_ref, li_ref, tfac_ref, nmat_ref):
     limat = li_ref[...]
     nmat_ref[...] = dot_tn(limat, uit_ref[...])
-    tful = -dot_nt(dot_nt(umat, rit_ref[...]), limat)
+    tful = -dot_nt(dot_nt(u_ref[...], rit_ref[...]), limat)
     rows = lax.broadcasted_iota(jnp.int32, (NC, NC), 0)
     cols = lax.broadcasted_iota(jnp.int32, (NC, NC), 1)
     tful = jnp.where(cols > rows, tful, 0.0)
-    tful = jnp.where(cols == rows, jnp.broadcast_to(tau_row[0:1], (NC, NC)), tful)
+    tful = jnp.where(cols == rows, jnp.broadcast_to(tau8_ref[0:1, :], (NC, NC)), tful)
     for j in range(PANELS):
         tfac_ref[j] = tful[j * BW:(j + 1) * BW, j * BW:(j + 1) * BW]
 
 
 def factor(gram, ptop):
     sq = jax.ShapeDtypeStruct((NC, NC), jnp.float32)
+    vm = pl.BlockSpec(memory_space=pltpu.VMEM)
+    tau = jax.ShapeDtypeStruct((1, NC), jnp.float32)
     return pl.pallas_call(
         factor_kernel,
-        out_shape=(sq, jax.ShapeDtypeStruct((PANELS, BW, BW), jnp.float32), jax.ShapeDtypeStruct((1, NC), jnp.float32), sq, sq, sq),
-        in_specs=[pl.BlockSpec(memory_space=pltpu.VMEM)] * 2,
-        out_specs=tuple([pl.BlockSpec(memory_space=pltpu.VMEM)] * 6),
-        scratch_shapes=[pltpu.VMEM((NC, NC), jnp.float32)] * 3,
+        out_shape=(sq, tau, jax.ShapeDtypeStruct((8, NC), jnp.float32), sq, sq, sq, sq),
+        in_specs=[vm] * 2,
+        out_specs=(vm,) * 7,
+        scratch_shapes=[pltpu.VMEM((NC, 2 * NC), jnp.float32)] * 3 + [pltpu.VMEM((NC, NC), jnp.float32)] * 2,
         compiler_params=pltpu.CompilerParams(vmem_limit_bytes=8 * 1024 * 1024),
-        cost_estimate=pl.CostEstimate(flops=400_000_000, bytes_accessed=600_000, transcendentals=0),
+        cost_estimate=pl.CostEstimate(flops=1_000_000_000, bytes_accessed=600_000, transcendentals=0),
         name="factor",
     )(gram, ptop)
+
+
+def finish(tau8, rit, uit, u, li):
+    vm = pl.BlockSpec(memory_space=pltpu.VMEM)
+    return pl.pallas_call(
+        finish_kernel,
+        out_shape=(jax.ShapeDtypeStruct((PANELS, BW, BW), jnp.float32), jax.ShapeDtypeStruct((NC, NC), jnp.float32)),
+        in_specs=[vm] * 5,
+        out_specs=(vm,) * 2,
+        compiler_params=pltpu.CompilerParams(vmem_limit_bytes=4 * 1024 * 1024),
+        cost_estimate=pl.CostEstimate(flops=300_000_000, bytes_accessed=400_000, transcendentals=0),
+        name="finish",
+    )(tau8, rit, uit, u, li)
 
 
 def gather_kernel(at_ref, a_v, pt_out, xh_out, g_out, ptop_out, head_out,
@@ -230,6 +252,12 @@
     x_v[...] = jnp.zeros_like(x_v)
     g_v[...] = jnp.zeros_like(g_v)
 
+    g_copies = []
+    for d in range(1, 4):
+        g_copies.append(pltpu.make_async_remote_copy(
+            src_ref=g_v, dst_ref=g_in.at[d - 1], send_sem=gsend.at[d - 1], recv_sem=grecv.at[d - 1],
+            device_id={'row': (r + d) % 4}, device_id_type=MESH))
+
     def chunk(c, carry):
         @pl.when(c + AHEAD < nch)
         def _():
@@ -264,8 +292,14 @@
 
         a_load(c).wait()
         p = pt_v[c].reshape(NC, CH)
+        g_v[...] += dot_nt(p, p)
+
+        @pl.when(c == nch - 1)
+        def _():
+            for g_copy in g_copies:
+                g_copy.start()
+
         x_v[...] += dot_nt(a_v[c], p)
-        g_v[...] += dot_nt(p, p)
         return carry
 
     lax.fori_loop(0, nch, chunk, 0)
@@ -276,13 +310,6 @@
         src_ref=x_v.at[pl.ds(half * (1 - core), half)], dst_ref=x_in, send_sem=xsend, recv_sem=xrecv,
         device_id={'row': mate}, device_id_type=MESH)
     x_copy.start()
-    g_copies = []
-    for d in range(1, 4):
-        g_copies.append(pltpu.make_async_remote_copy(
-            src_ref=g_v, dst_ref=g_in.at[d - 1], send_sem=gsend.at[d - 1], recv_sem=grecv.at[d - 1],
-            device_id={'row': (r + d) % 4}, device_id_type=MESH))
-        g_copies[-1].start()
-
     @pl.when(r == 0)
     def _():
         for p in range(1, 4):
@@ -347,14 +374,6 @@
     )(at)
 
 
-def split3(x):
-    hi = x.astype(jnp.bfloat16)
-    rem = x - hi.astype(jnp.float32)
-    mid = rem.astype(jnp.bfloat16)
-    lo = (rem - mid.astype(jnp.float32)).astype(jnp.bfloat16)
-    return hi, mid, lo
-
-
 def store_split(dst, rows, z):
     zh, zm, zl = split3(z)
     for i, part in enumerate((zh, zm, zh, zm, zh, zl)):
@@ -417,8 +436,11 @@
         ncol = local_blocks * bw
         at = a_local.transpose(1, 2, 0).reshape(ncol, local_rows)
         a, pt, xh, gram, ptop, head = gather(at)
-        x1, x2, x3 = [lax.ppermute(xh, 'row', [(i, i ^ b) for i in range(4)]) for b in (2, 1, 3)]
-        facet, tfac, tau, rit, nmat, uit = factor(gram, ptop)
+        x1, x2 = [lax.ppermute(xh, 'row', [(i, i ^ b) for i in range(4)]) for b in (2, 1)]
+        facet, tau, tau8, rit, uit, u, li = factor(gram, ptop)
+        x1, u = lax.optimization_barrier((x1, u))
+        x3 = lax.ppermute(x1, 'row', [(i, i ^ 1) for i in range(4)])
+        tfac, nmat = finish(tau8, rit, uit, u, li)
         out = update(a, pt, (xh, x1, x2, x3), head, rit, nmat, uit, facet)
         a_out = out.reshape(local_blocks, bw, local_rows).transpose(2, 0, 1)
         return a_out, tau.reshape(NC), tfac

time: 83.9 us -> 72.8 us (0.87)
  Pallas kernels: 80.9 us -> 70.2 us
  starting transfers between devices: 2.22 us -> 0.83 us
  waiting for transfers between devices: 0.01 us -> 0.9 us
    pallas_call x1 -> x2, Pallas kernels: 17.6 us -> 8.6 us  [the longest x1 7.22 us: factor(): pl.pallas_call(factor_kernel, out_shape=(sq, tau, jax.ShapeDtypeStruct((8...]
    pallas_call x1, Pallas kernels: 50.9 us -> 49.4 us  [gather(): pl.pallas_call(gather_kernel, out_shape=(jax.ShapeDtypeStruct((nch, ncol,...]
    ppermute x3 -> x2, starting transfers between devices: 2.22 us -> 0.83 us  [device_fn(): lax.ppermute(xh, 'row', [(i, i ^ b) for i in range(4)])]
  transfers between devices with their start and end apart: 3 -> 3, of which waited for: 0 -> 2; matrix products, arithmetic and copies ran while one was open for 0% -> 0% of each run, Pallas kernels for 21% -> 12%
where the time goes in v5:
time: 72.8 us; the launch traced here: 72.6 us
  Pallas kernels  70.2 us (96%)
  waiting for transfers between devices  0.9 us (1%)
  starting transfers between devices  0.83 us (1%)
    pallas_call x1, Pallas kernels, gather(): pl.pallas_call(gather_kernel, out_shape=(jax.ShapeDtypeStruct((nch, ncol,...  49.4 us
    pallas_call x1, Pallas kernels, update(): pl.pallas_call(update_kernel, grid=(nch,), out_shape=jax.ShapeDtypeStruct...  12.2 us
    pallas_call x1, Pallas kernels, factor(): pl.pallas_call(factor_kernel, out_shape=(sq, tau, jax.ShapeDtypeStruct((8...  7.22 us
  transfers between devices with their start and end apart: 3, of which 2 were waited for; matrix products, arithmetic and copies ran while one was open for 0% of the time, Pallas kernels for 12%

profile of v5, /device:TPU:0, one launch (start us, length us, event | category | flops | bytes accessed | tf_op | source)
XLA Modules:
  0.0 72.6 jit_solution(871862030038287249)
XLA Ops:
  0.6 49.4 %gather.1 = (f32[8,1024,512]{2,1,0:T(8,128)S(1)}, f32[8,4,32,512]{3,2,1,0:T(8,128)S(1)}, f32[512,128]{1,0:T(8,128)S(1)}, f32[128,128]{1,0:T(8,128)S(1)}, f32[128...) custom-call(f32[1024,4096]{1,0:T(8,128)} %bitcast.7), custom_call_target="tpu_custom_call" | custom-call | tf_op jit(solution)/shard_map/gather/pallas_call | solution.py:361
  50.0 0.7 %collective-permute-start = (f32[512,128]{1,0:T(8,128)S(1)}, f32[512,128]{1,0:T(8,128)S(1)}, u32[]{:S(2)}, u32[]{:S(2)}) collective-permute-start(f32[512,128]{1,0:T(8,128)S(1)} %get-tuple-element.22.x0_ref), channel_id=1, source_target_pairs={{0,2},{1,3},{2,0},{3,1},{4,6},{5,7},{6,4},{7,5},{8,10},{9,11},{10,... | collective-permute-start | bytes 786440 | tf_op jit(solution)/shard_map/ppermute | solution.py:439
  50.8 0.1 collective-permute-start.1
  50.9 7.2 %factor.1 = (f32[128,128]{1,0:T(8,128)S(1)}, f32[1,128]{1,0:T(1,128)}, f32[8,128]{1,0:T(8,128)S(1)}, f32[128,128]{1,0:T(8,128)S(1)}, f32[128,128]{1,0:T(8,128)S(...) custom-call(f32[128,128]{1,0:T(8,128)S(1)} %get-tuple-element.23.g_ref, f32[128,128]{1,0:T(8,128)S(1)} %get-tuple-element.24.ptop_ref), custom_call_target="tpu_custom_call" | custom-call | flops 1000000000 | bytes 600000 | tf_op jit(solution)/shard_map/factor/pallas_call | solution.py:152
  58.1 0.8 %collective-permute-done.x1_ref = f32[512,128]{1,0:T(8,128)S(1)} collective-permute-done((f32[512,128]{1,0:T(8,128)S(1)}, f32[512,128]{1,0:T(8,128)S(1)}, u32[]{:S(2)}, u32[]{:S(2)}) %collective-permute-start) | collective-permute-done | bytes 262176 | tf_op jit(solution)/shard_map/ppermute | solution.py:439
  58.8 0.0 collective-permute-start.2
  58.8 1.4 %finish.1 = (f32[4,32,32]{2,1,0:T(8,128)}, f32[128,128]{1,0:T(8,128)S(1)}) custom-call(f32[8,128]{1,0:T(8,128)S(1)} %get-tuple-element.29.tau8_ref, f32[128,128]{1,0:T(8,128)S(1)} %get-tuple-element.28.rit_ref, f32[128,128]{1,0:T(8,128)S(1)} %get-tuple-element.30.uit_ref, f32[128,128]{1,0:T(8,128)S(1)} %get-tuple-element.31.u_ref, ...), custom_call_target="tpu_custom_call" | custom-call | flops 300000000 | bytes 400000 | tf_op jit(solution)/shard_map/finish/pallas_call | solution.py:166
  60.2 0.0 collective-permute-done.1.x2_ref
  60.2 0.1 collective-permute-done.2.x3_ref
  60.4 12.2 %update.1 = f32[1024,4096]{1,0:T(8,128)} custom-call(f32[8,1024,512]{2,1,0:T(8,128)S(1)} %get-tuple-element.20.a_ref, f32[8,4,32,512]{3,2,1,0:T(8,128)S(1)} %get-tuple-element.21.pt_ref, f32[512,128]{1,0:T(8,128)S(1)} %get-tuple-element.22.x0_ref, f32[512,128]{1,0:T(8,128)S(1)} %collective-permute-done.x1_ref, f32[512,128]{1,0:T(8,128)S(1)} %collective-permute-done.1.x2_ref, ...), custom_call_target="tpu_custom_call" | custom-call | tf_op jit(solution)/shard_map/update/pallas_call | solution.py:419
Async XLA Ops:
  50.0 8.8 %collective-permute-start = (f32[512,128]{1,0:T(8,128)S(1)}, f32[512,128]{1,0:T(8,128)S(1)}, u32[]{:S(2)}, u32[]{:S(2)}) collective-permute-start(f32[512,128]{1,0:T(8,128)S(1)} %get-tuple-element.22.x0_ref), channel_id=1, source_target_pairs={{0,2},{1,3},{2,0},{3,1},{4,6},{5,7},{6,4},{7,5},{8,10},{9,11},{10,... | collective-permute-start | bytes 786440 | tf_op jit(solution)/shard_map/ppermute | solution.py:439
  50.8 9.5 %collective-permute-start.1 = (f32[512,128]{1,0:T(8,128)S(1)}, f32[512,128]{1,0:T(8,128)S(1)}, u32[]{:S(2)}, u32[]{:S(2)}) collective-permute-start(f32[512,128]{1,0:T(8,128)S(1)} %get-tuple-element.22.x0_ref), channel_id=1, source_target_pairs={{0,1},{1,0},{2,3},{3,2},{4,5},{5,4},{6,7},{7,6},{8,9},{9,8},{10,11... | collective-permute-start | bytes 786440 | tf_op jit(solution)/shard_map/ppermute | solution.py:439
  58.8 1.5 %collective-permute-start.2 = (f32[512,128]{1,0:T(8,128)S(1)}, f32[512,128]{1,0:T(8,128)S(1)}, u32[]{:S(2)}, u32[]{:S(2)}) collective-permute-start(f32[512,128]{1,0:T(8,128)S(1)} %collective-permute-done.x1_ref), channel_id=1, source_target_pairs={{0,1},{1,0},{2,3},{3,2},{4,5},{5,4},{6,7},{7,6},{8,9},{9,8},{10,11... | collective-permute-start | bytes 786440 | tf_op jit(solution)/shard_map/ppermute | solution.py:442

commit v6 on v5

--- a/solution.py
+++ b/solution.py
@@ -12,21 +12,12 @@
 CH = 512
 UPDATE_VMEM = 32 * 1024 * 1024
 GATHER_VMEM = 32 * 1024 * 1024
-AHEAD = 3
 HIGHEST = lax.Precision.HIGHEST
 MESH = pl.DeviceIdType.MESH
 
 
-def dot_nn(x, y):
-    return lax.dot_general(x, y, (((1,), (0,)), ((), ())), precision=HIGHEST, preferred_element_type=jnp.float32)
-
-
 def dot_nt(x, y):
     return lax.dot_general(x, y, (((1,), (1,)), ((), ())), precision=HIGHEST, preferred_element_type=jnp.float32)
-
-
-def dot_tn(x, y):
-    return lax.dot_general(x, y, (((0,), (0,)), ((), ())), precision=HIGHEST, preferred_element_type=jnp.float32)
 
 
 def split3(x):
@@ -35,6 +26,20 @@
     mid = rem.astype(jnp.bfloat16)
     lo = (rem - mid.astype(jnp.float32)).astype(jnp.bfloat16)
     return hi, mid, lo
+
+
+def stack6(x, axis, order):
+    parts = split3(x)
+    return jnp.concatenate([parts[i] for i in order], axis=axis)
+
+
+LEFT, RIGHT = (0, 1, 0, 1, 0, 2), (0, 1, 1, 0, 2, 0)
+
+
+def dot6(x, y, dims):
+    left = stack6(x, dims[0], LEFT)
+    right = stack6(y, dims[1], RIGHT)
+    return lax.dot_general(left, right, (((dims[0],), (dims[1],)), ((), ())), preferred_element_type=jnp.float32)
 
 
 def outer48(x, y):
@@ -135,8 +140,8 @@
 
 def finish_kernel(tau8_ref, rit_ref, uit_ref, u_ref, li_ref, tfac_ref, nmat_ref):
     limat = li_ref[...]
-    nmat_ref[...] = dot_tn(limat, uit_ref[...])
-    tful = -dot_nt(dot_nt(u_ref[...], rit_ref[...]), limat)
+    nmat_ref[...] = dot6(limat.T, uit_ref[...], (1, 0))
+    tful = -dot6(dot6(u_ref[...], rit_ref[...], (1, 1)), limat, (1, 1))
     rows = lax.broadcasted_iota(jnp.int32, (NC, NC), 0)
     cols = lax.broadcasted_iota(jnp.int32, (NC, NC), 1)
     tful = jnp.where(cols > rows, tful, 0.0)
@@ -195,7 +200,9 @@
             src_ref=pt_v.at[c, j], dst_ref=pt_v.at[c, j], send_sem=sem, recv_sem=recv.at[c, j],
             device_id={'col': to}, device_id_type=MESH)
 
-    routes = ((q + 2, q + 2 <= last, 0), (q - 2, q >= 2, 1), (q + 1, q < last, 2), (q - 1, q > 0, 3))
+    at_end = jnp.logical_or(q == 0, q == last)
+    inward = jnp.where(q == 0, 1, -1)
+    routes = ((q + 2 * inward, at_end, 0), (q + inward, at_end, 1), (q + 1, jnp.logical_not(at_end), 0), (q - 1, jnp.logical_not(at_end), 1))
 
     def send_own(c):
         own_load(c).wait()
@@ -221,14 +228,15 @@
 
     barrier = pltpu.get_barrier_semaphore()
 
-    for to, valid, _ in routes:
+    for to, valid in ((q + 2, q + 2 <= last), (q - 2, q >= 2), (q + 1, q < last), (q - 1, q > 0)):
         @pl.when(valid)
         def _():
             pl.semaphore_signal(barrier, inc=1, device_id={'col': to}, device_id_type=MESH)
 
     for d in range(1, 4):
         pl.semaphore_signal(barrier, inc=1, device_id={'row': (r + d) % 4}, device_id_type=MESH)
-    inner = jnp.logical_and(q > 0, q < last)
+    inner = jnp.logical_not(at_end)
+    outward = jnp.where(q == 1, -1, 1)
 
     @pl.when(inner)
     def _():
@@ -238,7 +246,7 @@
     def _():
         pl.semaphore_wait(barrier, 5)
 
-    for c in range(min(AHEAD, nch)):
+    for c in range(nch):
         send_own(c)
 
     head_local = pltpu.make_async_copy(at_ref.at[:, pl.ds(0, NC)], head_v, h_sem)
@@ -259,27 +267,20 @@
             device_id={'row': (r + d) % 4}, device_id_type=MESH))
 
     def chunk(c, carry):
-        @pl.when(c + AHEAD < nch)
-        def _():
-            send_own(c + AHEAD)
-
-        for d in range(1, 4):
-            @pl.when(q >= d)
-            def _():
-                hop(c, q - d, q, fwd.at[c]).wait_recv()
-
-            @pl.when(q + d <= last)
-            def _():
-                hop(c, q + d, q, fwd.at[c]).wait_recv()
-
-            if d == 2:
-                @pl.when(q == last - 1)
-                def _():
-                    hop(c, 0, q + 1, fwd.at[c]).start()
-
-                @pl.when(q == 1)
-                def _():
-                    hop(c, last, q - 1, fwd.at[c]).start()
+        near, far = q - outward, q - 2 * outward
+
+        @pl.when(inner)
+        def _():
+            hop(c, near, q, fwd.at[c, 0]).wait_recv()
+            hop(c, near, q + outward, fwd.at[c, 0]).start()
+            hop(c, far, q, fwd.at[c, 1]).wait_recv()
+            hop(c, far, q + outward, fwd.at[c, 1]).start()
+            hop(c, q + outward, q, fwd.at[c, 0]).wait_recv()
+
+        @pl.when(at_end)
+        def _():
+            for d in range(1, 4):
+                hop(c, q + d * inward, q, fwd.at[c, 0]).wait_recv()
 
         pt_out[c] = pt_v[c]
 
@@ -334,7 +335,8 @@
 
         @pl.when(inner)
         def _():
-            hop(c, q, q, fwd.at[c]).wait_send()
+            for slot in range(2):
+                hop(c, q, q, fwd.at[c, slot]).wait_send()
 
         return carry
 
@@ -367,17 +369,11 @@
         scratch_shapes=[pltpu.VMEM((nch, PANELS, BW, CH), f32), pltpu.VMEM((ncol, NC), f32),
                         pltpu.VMEM((NC, NC), f32), pltpu.VMEM((3, NC, NC), f32), pltpu.VMEM((ncol // 2, NC), f32),
                         pltpu.VMEM((ncol, NC), f32), pltpu.VMEM((PANELS, BW, NC), f32),
-                        dma((nch,)), dma((nch,)), dma((nch, 4)), dma((nch,)), dma((nch, 4)), dma, dma((4,)), dma, dma((4,)), dma,
+                        dma((nch,)), dma((nch,)), dma((nch, 2)), dma((nch, 2)), dma((nch, 4)), dma, dma((4,)), dma, dma((4,)), dma,
                         dma((3,)), dma((3,)), dma, dma],
         compiler_params=pltpu.CompilerParams(collective_id=0, has_side_effects=True, vmem_limit_bytes=GATHER_VMEM),
         name="gather",
     )(at)
-
-
-def store_split(dst, rows, z):
-    zh, zm, zl = split3(z)
-    for i, part in enumerate((zh, zm, zh, zm, zh, zl)):
-        dst[rows, i * NC:(i + 1) * NC] = part
 
 
 def update_kernel(a_ref, pt_ref, x0_ref, x1_ref, x2_ref, x3_ref, head_ref, rit_ref, nmat_ref, uit_ref, facet_ref, out_ref, z_v, top_v):
@@ -395,15 +391,14 @@
         mine = pl.multiple_of(half * core, half)
         other = pl.multiple_of(half * (1 - core), half)
         for lo, xa, xb in ((mine, x0_ref, x1_ref), (other, x2_ref, x3_ref)):
-            r12t = dot_nt(xa[...] + xb[...], rit)
+            r12t = dot6(xa[...] + xb[...], rit, (1, 1))
             top_v[pl.ds(lo, half), :] = r12t
-            store_split(z_v, pl.ds(lo, half), dot_nn(head_ref[pl.ds(lo, half), :] - r12t, nmat))
+            z_v[pl.ds(lo, half), :] = stack6(dot6(head_ref[pl.ds(lo, half), :] - r12t, nmat, (1, 0)), 1, LEFT)
         own = pl.ds(pl.multiple_of(q * BW, BW), BW)
         top_v[0:BW, :] = facet_ref[own, :]
-        store_split(z_v, pl.ds(0, BW), -uit_ref[own, :])
-
-    ph, pm, plo = split3(pt_ref[step].reshape(NC, CH))
-    wide = jnp.concatenate([ph, pm, pm, ph, plo, ph], axis=0)
+        z_v[0:BW, :] = stack6(-uit_ref[own, :], 1, LEFT)
+
+    wide = stack6(pt_ref[step].reshape(NC, CH), 0, RIGHT)
     prod = lax.dot_general(z_v[...], wide, (((1,), (0,)), ((), ())), preferred_element_type=jnp.float32)
     out_ref[BW:, :] = a_ref[step, BW:, :] - prod[BW:]
     out_ref[0:BW, :] = -prod[0:BW]

time: 72.8 us -> 68.3 us (0.938)
  Pallas kernels: 70.2 us -> 65.7 us
    pallas_call x1, Pallas kernels: 49.4 us -> 45.5 us  [gather(): pl.pallas_call(gather_kernel, out_shape=(jax.ShapeDtypeStruct((nch, ncol,...]
where the time goes in v6:
time: 68.3 us; the launch traced here: 68.2 us
  Pallas kernels  65.7 us (96%)
  waiting for transfers between devices  1.03 us (2%)
  starting transfers between devices  0.83 us (1%)
    pallas_call x1, Pallas kernels, gather(): pl.pallas_call(gather_kernel, out_shape=(jax.ShapeDtypeStruct((nch, ncol,...  45.5 us
    pallas_call x1, Pallas kernels, update(): pl.pallas_call(update_kernel, grid=(nch,), out_shape=jax.ShapeDtypeStruct...  11.7 us
    pallas_call x1, Pallas kernels, factor(): pl.pallas_call(factor_kernel, out_shape=(sq, tau, jax.ShapeDtypeStruct((8...  7.21 us
  transfers between devices with their start and end apart: 3, of which 2 were waited for; matrix products, arithmetic and copies ran while one was open for 0% of the time, Pallas kernels for 12%

profile of v6, /device:TPU:0, one launch (start us, length us, event | category | flops | bytes accessed | tf_op | source)
XLA Modules:
  0.0 68.2 jit_solution(17629539325814534202)
XLA Ops:
  0.6 45.5 %gather.1 = (f32[8,1024,512]{2,1,0:T(8,128)S(1)}, f32[8,4,32,512]{3,2,1,0:T(8,128)S(1)}, f32[512,128]{1,0:T(8,128)S(1)}, f32[128,128]{1,0:T(8,128)S(1)}, f32[128...) custom-call(f32[1024,4096]{1,0:T(8,128)} %bitcast.7), custom_call_target="tpu_custom_call" | custom-call | tf_op jit(solution)/shard_map/gather/pallas_call | solution.py:363
  46.2 0.7 %collective-permute-start = (f32[512,128]{1,0:T(8,128)S(1)}, f32[512,128]{1,0:T(8,128)S(1)}, u32[]{:S(2)}, u32[]{:S(2)}) collective-permute-start(f32[512,128]{1,0:T(8,128)S(1)} %get-tuple-element.22.x0_ref), channel_id=1, source_target_pairs={{0,2},{1,3},{2,0},{3,1},{4,6},{5,7},{6,4},{7,5},{8,10},{9,11},{10,... | collective-permute-start | bytes 786440 | tf_op jit(solution)/shard_map/ppermute | solution.py:434
  46.9 0.1 collective-permute-start.1
  47.0 7.2 %factor.1 = (f32[128,128]{1,0:T(8,128)S(1)}, f32[1,128]{1,0:T(1,128)}, f32[8,128]{1,0:T(8,128)S(1)}, f32[128,128]{1,0:T(8,128)S(1)}, f32[128,128]{1,0:T(8,128)S(...) custom-call(f32[128,128]{1,0:T(8,128)S(1)} %get-tuple-element.23.g_ref, f32[128,128]{1,0:T(8,128)S(1)} %get-tuple-element.24.ptop_ref), custom_call_target="tpu_custom_call" | custom-call | flops 1000000000 | bytes 600000 | tf_op jit(solution)/shard_map/factor/pallas_call | solution.py:157
  54.2 0.8 %collective-permute-done.x1_ref = f32[512,128]{1,0:T(8,128)S(1)} collective-permute-done((f32[512,128]{1,0:T(8,128)S(1)}, f32[512,128]{1,0:T(8,128)S(1)}, u32[]{:S(2)}, u32[]{:S(2)}) %collective-permute-start) | collective-permute-done | bytes 262176 | tf_op jit(solution)/shard_map/ppermute | solution.py:434
  55.0 0.0 collective-permute-start.2
  55.0 1.3 %finish.1 = (f32[4,32,32]{2,1,0:T(8,128)}, f32[128,128]{1,0:T(8,128)S(1)}) custom-call(f32[8,128]{1,0:T(8,128)S(1)} %get-tuple-element.29.tau8_ref, f32[128,128]{1,0:T(8,128)S(1)} %get-tuple-element.28.rit_ref, f32[128,128]{1,0:T(8,128)S(1)} %get-tuple-element.30.uit_ref, f32[128,128]{1,0:T(8,128)S(1)} %get-tuple-element.31.u_ref, ...), custom_call_target="tpu_custom_call" | custom-call | flops 300000000 | bytes 400000 | tf_op jit(solution)/shard_map/finish/pallas_call | solution.py:171
  56.2 0.0 collective-permute-done.1.x2_ref
  56.2 0.3 collective-permute-done.2.x3_ref
  56.5 11.7 %update.1 = f32[1024,4096]{1,0:T(8,128)} custom-call(f32[8,1024,512]{2,1,0:T(8,128)S(1)} %get-tuple-element.20.a_ref, f32[8,4,32,512]{3,2,1,0:T(8,128)S(1)} %get-tuple-element.21.pt_ref, f32[512,128]{1,0:T(8,128)S(1)} %get-tuple-element.22.x0_ref, f32[512,128]{1,0:T(8,128)S(1)} %collective-permute-done.x1_ref, f32[512,128]{1,0:T(8,128)S(1)} %collective-permute-done.1.x2_ref, ...), custom_call_target="tpu_custom_call" | custom-call | tf_op jit(solution)/shard_map/update/pallas_call | solution.py:414
Async XLA Ops:
  46.2 8.8 %collective-permute-start = (f32[512,128]{1,0:T(8,128)S(1)}, f32[512,128]{1,0:T(8,128)S(1)}, u32[]{:S(2)}, u32[]{:S(2)}) collective-permute-start(f32[512,128]{1,0:T(8,128)S(1)} %get-tuple-element.22.x0_ref), channel_id=1, source_target_pairs={{0,2},{1,3},{2,0},{3,1},{4,6},{5,7},{6,4},{7,5},{8,10},{9,11},{10,... | collective-permute-start | bytes 786440 | tf_op jit(solution)/shard_map/ppermute | solution.py:434
  46.9 9.3 %collective-permute-start.1 = (f32[512,128]{1,0:T(8,128)S(1)}, f32[512,128]{1,0:T(8,128)S(1)}, u32[]{:S(2)}, u32[]{:S(2)}) collective-permute-start(f32[512,128]{1,0:T(8,128)S(1)} %get-tuple-element.22.x0_ref), channel_id=1, source_target_pairs={{0,1},{1,0},{2,3},{3,2},{4,5},{5,4},{6,7},{7,6},{8,9},{9,8},{10,11... | collective-permute-start | bytes 786440 | tf_op jit(solution)/shard_map/ppermute | solution.py:434
  55.0 1.5 %collective-permute-start.2 = (f32[512,128]{1,0:T(8,128)S(1)}, f32[512,128]{1,0:T(8,128)S(1)}, u32[]{:S(2)}, u32[]{:S(2)}) collective-permute-start(f32[512,128]{1,0:T(8,128)S(1)} %collective-permute-done.x1_ref), channel_id=1, source_target_pairs={{0,1},{1,0},{2,3},{3,2},{4,5},{5,4},{6,7},{7,6},{8,9},{9,8},{10,11... | collective-permute-start | bytes 786440 | tf_op jit(solution)/shard_map/ppermute | solution.py:437

commit v7 on v6

--- a/solution.py
+++ b/solution.py
@@ -179,7 +179,7 @@
     )(tau8, rit, uit, u, li)
 
 
-def gather_kernel(at_ref, a_v, pt_out, xh_out, g_out, ptop_out, head_out,
+def gather_kernel(at_ref, a_v, pt_out, xh_out, xo_out, g_out, ptop_out, head_out,
                   pt_v, x_v, g_v, g_in, x_in, head_v, ptop_v,
                   a_sem, own_sem, send, fwd, recv, h_sem, hsend, hrecv, psend, precv, gsend, grecv, xsend, xrecv):
     ncol, local_rows = at_ref.shape
@@ -308,7 +308,7 @@
     core = r % 2
     mate = r + 1 - 2 * core
     x_copy = pltpu.make_async_remote_copy(
-        src_ref=x_v.at[pl.ds(half * (1 - core), half)], dst_ref=x_in, send_sem=xsend, recv_sem=xrecv,
+        src_ref=x_v, dst_ref=x_in, send_sem=xsend, recv_sem=xrecv,
         device_id={'row': mate}, device_id_type=MESH)
     x_copy.start()
     @pl.when(r == 0)
@@ -351,7 +351,9 @@
         total = part if total is None else total + part
     g_out[...] = total
     x_copy.wait()
-    xh_out[...] = x_v[pl.ds(half * core, half), :] + x_in[...]
+    mine, other = pl.ds(half * core, half), pl.ds(half * (1 - core), half)
+    xh_out[...] = x_v[mine, :] + x_in[mine, :]
+    xo_out[...] = x_v[other, :] + x_in[other, :]
 
 
 def gather(at):
@@ -362,12 +364,12 @@
     dma = pltpu.SemaphoreType.DMA
     return pl.pallas_call(
         gather_kernel,
-        out_shape=(jax.ShapeDtypeStruct((nch, ncol, CH), f32), jax.ShapeDtypeStruct((nch, PANELS, BW, CH), f32), jax.ShapeDtypeStruct((ncol // 2, NC), f32),
+        out_shape=(jax.ShapeDtypeStruct((nch, ncol, CH), f32), jax.ShapeDtypeStruct((nch, PANELS, BW, CH), f32), jax.ShapeDtypeStruct((ncol // 2, NC), f32), jax.ShapeDtypeStruct((ncol // 2, NC), f32),
                    jax.ShapeDtypeStruct((NC, NC), f32), jax.ShapeDtypeStruct((NC, NC), f32), jax.ShapeDtypeStruct((ncol, NC), f32)),
         in_specs=[anys],
-        out_specs=(vm,) * 6,
+        out_specs=(vm,) * 7,
         scratch_shapes=[pltpu.VMEM((nch, PANELS, BW, CH), f32), pltpu.VMEM((ncol, NC), f32),
-                        pltpu.VMEM((NC, NC), f32), pltpu.VMEM((3, NC, NC), f32), pltpu.VMEM((ncol // 2, NC), f32),
+                        pltpu.VMEM((NC, NC), f32), pltpu.VMEM((3, NC, NC), f32), pltpu.VMEM((ncol, NC), f32),
                         pltpu.VMEM((ncol, NC), f32), pltpu.VMEM((PANELS, BW, NC), f32),
                         dma((nch,)), dma((nch,)), dma((nch, 2)), dma((nch, 2)), dma((nch, 4)), dma, dma((4,)), dma, dma((4,)), dma,
                         dma((3,)), dma((3,)), dma, dma],
@@ -376,36 +378,46 @@
     )(at)
 
 
-def update_kernel(a_ref, pt_ref, x0_ref, x1_ref, x2_ref, x3_ref, head_ref, rit_ref, nmat_ref, uit_ref, facet_ref, out_ref, z_v, top_v):
-    step = pl.program_id(0)
+def update_kernel(a_ref, pt_ref, x0_ref, x1_ref, x2_ref, x3_ref, head_ref, rit_ref, nmat_ref, uit_ref, facet_ref, out_ref, z_v, top_v, sem, *strips):
     q = lax.axis_index('col')
     r = lax.axis_index('row')
     ncol = head_ref.shape[0]
     half = ncol // 2
-
-    @pl.when(step == 0)
-    def _():
-        core = r % 2
-        rit = rit_ref[...]
-        nmat = nmat_ref[...]
-        mine = pl.multiple_of(half * core, half)
-        other = pl.multiple_of(half * (1 - core), half)
-        for lo, xa, xb in ((mine, x0_ref, x1_ref), (other, x2_ref, x3_ref)):
-            r12t = dot6(xa[...] + xb[...], rit, (1, 1))
-            top_v[pl.ds(lo, half), :] = r12t
-            z_v[pl.ds(lo, half), :] = stack6(dot6(head_ref[pl.ds(lo, half), :] - r12t, nmat, (1, 0)), 1, LEFT)
-        own = pl.ds(pl.multiple_of(q * BW, BW), BW)
-        top_v[0:BW, :] = facet_ref[own, :]
-        z_v[0:BW, :] = stack6(-uit_ref[own, :], 1, LEFT)
-
-    wide = stack6(pt_ref[step].reshape(NC, CH), 0, RIGHT)
-    prod = lax.dot_general(z_v[...], wide, (((1,), (0,)), ((), ())), preferred_element_type=jnp.float32)
-    out_ref[BW:, :] = a_ref[step, BW:, :] - prod[BW:]
-    out_ref[0:BW, :] = -prod[0:BW]
-
-    @pl.when(jnp.logical_and(step == 0, r == 0))
-    def _():
-        out_ref[:, 0:NC] = top_v[...]
+    core = r % 2
+    rit = rit_ref[...]
+    nmat = nmat_ref[...]
+    mine = pl.multiple_of(half * core, half)
+    other = pl.multiple_of(half * (1 - core), half)
+    for lo, xa, xb in ((mine, x0_ref, x1_ref), (other, x2_ref, x3_ref)):
+        r12t = dot6(xa[...] + xb[...], rit, (1, 1))
+        top_v[pl.ds(lo, half), :] = r12t
+        z_v[pl.ds(lo, half), :] = stack6(dot6(head_ref[pl.ds(lo, half), :] - r12t, nmat, (1, 0)), 1, LEFT)
+    own = pl.ds(pl.multiple_of(q * BW, BW), BW)
+    top_v[0:BW, :] = facet_ref[own, :]
+    z_v[0:BW, :] = stack6(-uit_ref[own, :], 1, LEFT)
+
+    copies = []
+    for step, strip in enumerate(strips):
+        wide = stack6(pt_ref[step].reshape(NC, CH), 0, RIGHT)
+        parts = 2 if step == len(strips) - 1 else 1
+        size = ncol // parts
+        for part in range(parts):
+            lo = part * size
+            prod = lax.dot_general(z_v[lo:lo + size, :], wide, (((1,), (0,)), ((), ())), preferred_element_type=jnp.float32)
+            if part == 0:
+                new = jnp.concatenate([-prod[0:BW], a_ref[step, BW:size, :] - prod[BW:]], axis=0)
+            else:
+                new = a_ref[step, lo:lo + size, :] - prod
+            if step == 0:
+                strip[:, 0:NC] = jnp.where(r == 0, top_v[...], new[:, 0:NC])
+                strip[:, NC:] = new[:, NC:]
+            else:
+                strip[lo:lo + size, :] = new
+            copies.append(pltpu.make_async_copy(
+                strip.at[pl.ds(lo, size)], out_ref.at[pl.ds(lo, size), pl.ds(step * CH, CH)], sem.at[len(copies)]))
+            copies[-1].start()
+    for copy in copies:
+        copy.wait()
 
 
 def update(a, pt, xs, head, rit, nmat, uit, facet):
@@ -413,12 +425,12 @@
     vm = pl.BlockSpec(memory_space=pltpu.VMEM)
     return pl.pallas_call(
         update_kernel,
-        grid=(nch,),
         out_shape=jax.ShapeDtypeStruct((ncol, nch * CH), jnp.float32),
         in_specs=[vm] * 11,
-        out_specs=pl.BlockSpec((ncol, CH), lambda i: (0, i)),
-        scratch_shapes=[pltpu.VMEM((ncol, 6 * NC), jnp.bfloat16), pltpu.VMEM((ncol, NC), jnp.float32)],
-        compiler_params=pltpu.CompilerParams(dimension_semantics=("arbitrary",), vmem_limit_bytes=UPDATE_VMEM),
+        out_specs=pl.BlockSpec(memory_space=pl.ANY),
+        scratch_shapes=[pltpu.VMEM((ncol, 6 * NC), jnp.bfloat16), pltpu.VMEM((ncol, NC), jnp.float32), pltpu.SemaphoreType.DMA((nch + 1,))]
+        + [pltpu.VMEM((ncol, CH), jnp.float32)] * nch,
+        compiler_params=pltpu.CompilerParams(vmem_limit_bytes=UPDATE_VMEM),
         name="update",
     )(a, pt, *xs, head, rit, nmat, uit, facet)
 
@@ -430,13 +442,13 @@
         local_rows, local_blocks, bw = a_local.shape
         ncol = local_blocks * bw
         at = a_local.transpose(1, 2, 0).reshape(ncol, local_rows)
-        a, pt, xh, gram, ptop, head = gather(at)
-        x1, x2 = [lax.ppermute(xh, 'row', [(i, i ^ b) for i in range(4)]) for b in (2, 1)]
+        a, pt, xh, xo, gram, ptop, head = gather(at)
+        x1 = lax.ppermute(xh, 'row', [(i, i ^ 2) for i in range(4)])
         facet, tau, tau8, rit, uit, u, li = factor(gram, ptop)
         x1, u = lax.optimization_barrier((x1, u))
         x3 = lax.ppermute(x1, 'row', [(i, i ^ 1) for i in range(4)])
         tfac, nmat = finish(tau8, rit, uit, u, li)
-        out = update(a, pt, (xh, x1, x2, x3), head, rit, nmat, uit, facet)
+        out = update(a, pt, (xh, x1, xo, x3), head, rit, nmat, uit, facet)
         a_out = out.reshape(local_blocks, bw, local_rows).transpose(2, 0, 1)
         return a_out, tau.reshape(NC), tfac
 

time: 68.3 us -> 67.8 us (level)
  Pallas kernels: 65.7 us -> 65 us
    pallas_call x1, Pallas kernels: 11.7 us -> 11 us  [update(): pl.pallas_call(update_kernel, out_shape=jax.ShapeDtypeStruct((ncol, nch *...]
  transfers between devices with their start and end apart: 3 -> 2, of which waited for: 2 -> 2; matrix products, arithmetic and copies ran while one was open for 0% -> 0% of each run, Pallas kernels for 12% -> 13%
where the time goes in v7:
time: 67.8 us; the launch traced here: 67.7 us
  Pallas kernels  65 us (96%)
  starting transfers between devices  1.11 us (2%)
  between operations  0.8 us (1%)
  waiting for transfers between devices  0.74 us (1%)
    pallas_call x1, Pallas kernels, gather(): pl.pallas_call(gather_kernel, out_shape=(jax.ShapeDtypeStruct((nch, ncol,...  45.6 us
    pallas_call x1, Pallas kernels, update(): pl.pallas_call(update_kernel, out_shape=jax.ShapeDtypeStruct((ncol, nch *...  11 us
    pallas_call x1, Pallas kernels, factor(): pl.pallas_call(factor_kernel, out_shape=(sq, tau, jax.ShapeDtypeStruct((8...  7.21 us
  transfers between devices with their start and end apart: 2, of which 2 were waited for; matrix products, arithmetic and copies ran while one was open for 0% of the time, Pallas kernels for 13%

profile of v7, /device:TPU:0, one launch (start us, length us, event | category | flops | bytes accessed | tf_op | source)
XLA Modules:
  0.0 67.7 jit_solution(13144545862935476420)
XLA Ops:
  0.6 45.6 %gather.1 = (f32[8,1024,512]{2,1,0:T(8,128)S(1)}, f32[8,4,32,512]{3,2,1,0:T(8,128)S(1)}, f32[512,128]{1,0:T(8,128)S(1)}, f32[512,128]{1,0:T(8,128)S(1)}, f32[128...) custom-call(f32[1024,4096]{1,0:T(8,128)} %bitcast.7), custom_call_target="tpu_custom_call" | custom-call | tf_op jit(solution)/shard_map/gather/pallas_call | solution.py:365
  46.2 1.1 %collective-permute-start = (f32[512,128]{1,0:T(8,128)S(1)}, f32[512,128]{1,0:T(8,128)S(1)}, u32[]{:S(2)}, u32[]{:S(2)}) collective-permute-start(f32[512,128]{1,0:T(8,128)S(1)} %get-tuple-element.23.x0_ref), channel_id=1, source_target_pairs={{0,2},{1,3},{2,0},{3,1},{4,6},{5,7},{6,4},{7,5},{8,10},{9,11},{10,... | collective-permute-start | bytes 786440 | tf_op jit(solution)/shard_map/ppermute | solution.py:446
  47.3 7.2 %factor.1 = (f32[128,128]{1,0:T(8,128)S(1)}, f32[1,128]{1,0:T(1,128)}, f32[8,128]{1,0:T(8,128)S(1)}, f32[128,128]{1,0:T(8,128)S(1)}, f32[128,128]{1,0:T(8,128)S(...) custom-call(f32[128,128]{1,0:T(8,128)S(1)} %get-tuple-element.24.g_ref, f32[128,128]{1,0:T(8,128)S(1)} %get-tuple-element.25.ptop_ref), custom_call_target="tpu_custom_call" | custom-call | flops 1000000000 | bytes 600000 | tf_op jit(solution)/shard_map/factor/pallas_call | solution.py:157
  54.5 0.5 collective-permute-done.x1_ref
  55.0 0.0 collective-permute-start.1
  55.0 1.3 %finish.1 = (f32[4,32,32]{2,1,0:T(8,128)}, f32[128,128]{1,0:T(8,128)S(1)}) custom-call(f32[8,128]{1,0:T(8,128)S(1)} %get-tuple-element.31.tau8_ref, f32[128,128]{1,0:T(8,128)S(1)} %get-tuple-element.30.rit_ref, f32[128,128]{1,0:T(8,128)S(1)} %get-tuple-element.32.uit_ref, f32[128,128]{1,0:T(8,128)S(1)} %get-tuple-element.33.u_ref, ...), custom_call_target="tpu_custom_call" | custom-call | flops 300000000 | bytes 400000 | tf_op jit(solution)/shard_map/finish/pallas_call | solution.py:171
  56.3 0.3 collective-permute-done.1.x3_ref
  56.5 11.0 %update.1 = f32[1024,4096]{1,0:T(8,128)} custom-call(f32[8,1024,512]{2,1,0:T(8,128)S(1)} %get-tuple-element.21.a_ref, f32[8,4,32,512]{3,2,1,0:T(8,128)S(1)} %get-tuple-element.22.pt_ref, f32[512,128]{1,0:T(8,128)S(1)} %get-tuple-element.23.x0_ref, f32[512,128]{1,0:T(8,128)S(1)} %collective-permute-done.x1_ref, f32[512,128]{1,0:T(8,128)S(1)} %get-tuple-element.28.x2_ref, ...), custom_call_target="tpu_custom_call" | custom-call | tf_op jit(solution)/shard_map/update/pallas_call | solution.py:426
Async XLA Ops:
  46.2 8.8 %collective-permute-start = (f32[512,128]{1,0:T(8,128)S(1)}, f32[512,128]{1,0:T(8,128)S(1)}, u32[]{:S(2)}, u32[]{:S(2)}) collective-permute-start(f32[512,128]{1,0:T(8,128)S(1)} %get-tuple-element.23.x0_ref), channel_id=1, source_target_pairs={{0,2},{1,3},{2,0},{3,1},{4,6},{5,7},{6,4},{7,5},{8,10},{9,11},{10,... | collective-permute-start | bytes 786440 | tf_op jit(solution)/shard_map/ppermute | solution.py:446
  55.0 1.5 %collective-permute-start.1 = (f32[512,128]{1,0:T(8,128)S(1)}, f32[512,128]{1,0:T(8,128)S(1)}, u32[]{:S(2)}, u32[]{:S(2)}) collective-permute-start(f32[512,128]{1,0:T(8,128)S(1)} %collective-permute-done.x1_ref), channel_id=1, source_target_pairs={{0,1},{1,0},{2,3},{3,2},{4,5},{5,4},{6,7},{7,6},{8,9},{9,8},{10,11... | collective-permute-start | bytes 786440 | tf_op jit(solution)/shard_map/ppermute | solution.py:449

commit v8 on v7

--- a/solution.py
+++ b/solution.py
@@ -18,6 +18,10 @@
 
 def dot_nt(x, y):
     return lax.dot_general(x, y, (((1,), (1,)), ((), ())), precision=HIGHEST, preferred_element_type=jnp.float32)
+
+
+def dot16_nt(x, y):
+    return lax.dot_general(x, y, (((1,), (1,)), ((), ())), preferred_element_type=jnp.float32)
 
 
 def split3(x):
@@ -180,7 +184,7 @@
 
 
 def gather_kernel(at_ref, a_v, pt_out, xh_out, xo_out, g_out, ptop_out, head_out,
-                  pt_v, x_v, g_v, g_in, x_in, head_v, ptop_v,
+                  pt_v, x_v, g_v, g_in, g_sum, g_end, x_in, head_v, ptop_v,
                   a_sem, own_sem, send, fwd, recv, h_sem, hsend, hrecv, psend, precv, gsend, grecv, xsend, xrecv):
     ncol, local_rows = at_ref.shape
     nch = local_rows // CH
@@ -293,14 +297,21 @@
 
         a_load(c).wait()
         p = pt_v[c].reshape(NC, CH)
-        g_v[...] += dot_nt(p, p)
-
-        @pl.when(c == nch - 1)
+        @pl.when(inner)
+        def _():
+            g_v[...] += dot_nt(p, p)
+
+        @pl.when(jnp.logical_and(c == nch - 1, inner))
         def _():
             for g_copy in g_copies:
                 g_copy.start()
 
-        x_v[...] += dot_nt(a_v[c], p)
+        ah, am, al = split3(a_v[c])
+        ph, pm, plo = split3(p)
+        both = jnp.concatenate([ph, pm], axis=0)
+        main = dot16_nt(ah, both) + dot16_nt(am, both)
+        low = dot16_nt(jnp.concatenate([ah, al], axis=1), jnp.concatenate([plo, ph], axis=1))
+        x_v[...] += main[:, 0:NC] + (main[:, NC:] + low)
         return carry
 
     lax.fori_loop(0, nch, chunk, 0)
@@ -311,6 +322,17 @@
         src_ref=x_v, dst_ref=x_in, send_sem=xsend, recv_sem=xrecv,
         device_id={'row': mate}, device_id_type=MESH)
     x_copy.start()
+
+    part = pl.ds((NC // 2) * core, NC // 2)
+
+    def half_copy(to):
+        return pltpu.make_async_remote_copy(
+            src_ref=g_sum.at[part], dst_ref=g_end.at[part], send_sem=gsend.at[3], recv_sem=grecv.at[3],
+            device_id={'col': to}, device_id_type=MESH)
+
+    mate_copy = pltpu.make_async_remote_copy(
+        src_ref=g_end.at[part], dst_ref=g_end.at[part], send_sem=gsend.at[4], recv_sem=grecv.at[4],
+        device_id={'row': mate}, device_id_type=MESH)
     @pl.when(r == 0)
     def _():
         for p in range(1, 4):
@@ -341,19 +363,38 @@
         return carry
 
     lax.fori_loop(0, nch, drain, 0)
-    for g_copy in g_copies:
-        g_copy.wait()
-    parts = [g_v[...]] + [g_in[d - 1] for d in range(1, 4)]
-    total = None
-    for row in range(4):
-        dist = (r - row + 4) % 4
-        part = jnp.where(dist == 0, parts[0], jnp.where(dist == 1, parts[1], jnp.where(dist == 2, parts[2], parts[3])))
-        total = part if total is None else total + part
-    g_out[...] = total
+    @pl.when(inner)
+    def _():
+        for g_copy in g_copies:
+            g_copy.wait()
+        parts = [g_v[...]] + [g_in[d - 1] for d in range(1, 4)]
+        total = None
+        for row in range(4):
+            dist = (r - row + 4) % 4
+            part = jnp.where(dist == 0, parts[0], jnp.where(dist == 1, parts[1], jnp.where(dist == 2, parts[2], parts[3])))
+            total = part if total is None else total + part
+        g_out[...] = total
+        g_sum[...] = total
+
+    @pl.when(at_end)
+    def _():
+        half_copy(q).wait_recv()
+        mate_copy.start()
+
     x_copy.wait()
     mine, other = pl.ds(half * core, half), pl.ds(half * (1 - core), half)
     xh_out[...] = x_v[mine, :] + x_in[mine, :]
     xo_out[...] = x_v[other, :] + x_in[other, :]
+
+    @pl.when(inner)
+    def _():
+        half_copy(q + outward).start()
+        half_copy(q + outward).wait_send()
+
+    @pl.when(at_end)
+    def _():
+        mate_copy.wait()
+        g_out[...] = g_end[...]
 
 
 def gather(at):
@@ -369,10 +410,10 @@
         in_specs=[anys],
         out_specs=(vm,) * 7,
         scratch_shapes=[pltpu.VMEM((nch, PANELS, BW, CH), f32), pltpu.VMEM((ncol, NC), f32),
-                        pltpu.VMEM((NC, NC), f32), pltpu.VMEM((3, NC, NC), f32), pltpu.VMEM((ncol, NC), f32),
+                        pltpu.VMEM((NC, NC), f32), pltpu.VMEM((3, NC, NC), f32), pltpu.VMEM((NC, NC), f32), pltpu.VMEM((NC, NC), f32), pltpu.VMEM((ncol, NC), f32),
                         pltpu.VMEM((ncol, NC), f32), pltpu.VMEM((PANELS, BW, NC), f32),
                         dma((nch,)), dma((nch,)), dma((nch, 2)), dma((nch, 2)), dma((nch, 4)), dma, dma((4,)), dma, dma((4,)), dma,
-                        dma((3,)), dma((3,)), dma, dma],
+                        dma((5,)), dma((5,)), dma, dma],
         compiler_params=pltpu.CompilerParams(collective_id=0, has_side_effects=True, vmem_limit_bytes=GATHER_VMEM),
         name="gather",
     )(at)

time: 67.8 us -> 66.5 us (0.981)
  Pallas kernels: 65 us -> 63.7 us
    pallas_call x1, Pallas kernels: 45.6 us -> 44.2 us  [gather(): pl.pallas_call(gather_kernel, out_shape=(jax.ShapeDtypeStruct((nch, ncol,...]
  transfers between devices with their start and end apart: 2 -> 2, of which waited for: 2 -> 1; matrix products, arithmetic and copies ran while one was open for 0% -> 0% of each run, Pallas kernels for 13% -> 13%
where the time goes in v8:
time: 66.5 us; the launch traced here: 66.3 us
  Pallas kernels  63.7 us (96%)
  starting transfers between devices  1.67 us (3%)
  between operations  0.8 us (1%)
    pallas_call x1, Pallas kernels, gather(): pl.pallas_call(gather_kernel, out_shape=(jax.ShapeDtypeStruct((nch, ncol,...  44.2 us
    pallas_call x1, Pallas kernels, update(): pl.pallas_call(update_kernel, out_shape=jax.ShapeDtypeStruct((ncol, nch *...  11 us
    pallas_call x1, Pallas kernels, factor(): pl.pallas_call(factor_kernel, out_shape=(sq, tau, jax.ShapeDtypeStruct((8...  7.22 us
    ppermute x1, starting transfers between devices, device_fn(): x1 = lax.ppermute(xh, 'row', [(i, i ^ 2) for i in range(4)])  1.59 us
  transfers between devices with their start and end apart: 2, of which 1 were waited for; matrix products, arithmetic and copies ran while one was open for 0% of the time, Pallas kernels for 13%

profile of v8, /device:TPU:0, one launch (start us, length us, event | category | flops | bytes accessed | tf_op | source)
XLA Modules:
  0.0 66.3 jit_solution(1604939399264471617)
XLA Ops:
  0.6 44.2 %gather.1 = (f32[8,1024,512]{2,1,0:T(8,128)S(1)}, f32[8,4,32,512]{3,2,1,0:T(8,128)S(1)}, f32[512,128]{1,0:T(8,128)S(1)}, f32[512,128]{1,0:T(8,128)S(1)}, f32[128...) custom-call(f32[1024,4096]{1,0:T(8,128)} %bitcast.7), custom_call_target="tpu_custom_call" | custom-call | tf_op jit(solution)/shard_map/gather/pallas_call | solution.py:406
  44.9 1.6 %collective-permute-start = (f32[512,128]{1,0:T(8,128)S(1)}, f32[512,128]{1,0:T(8,128)S(1)}, u32[]{:S(2)}, u32[]{:S(2)}) collective-permute-start(f32[512,128]{1,0:T(8,128)S(1)} %get-tuple-element.23.x0_ref), channel_id=1, source_target_pairs={{0,2},{1,3},{2,0},{3,1},{4,6},{5,7},{6,4},{7,5},{8,10},{9,11},{10,... | collective-permute-start | bytes 786440 | tf_op jit(solution)/shard_map/ppermute | solution.py:487
  46.5 7.2 %factor.1 = (f32[128,128]{1,0:T(8,128)S(1)}, f32[1,128]{1,0:T(1,128)}, f32[8,128]{1,0:T(8,128)S(1)}, f32[128,128]{1,0:T(8,128)S(1)}, f32[128,128]{1,0:T(8,128)S(...) custom-call(f32[128,128]{1,0:T(8,128)S(1)} %get-tuple-element.24.g_ref, f32[128,128]{1,0:T(8,128)S(1)} %get-tuple-element.25.ptop_ref), custom_call_target="tpu_custom_call" | custom-call | flops 1000000000 | bytes 600000 | tf_op jit(solution)/shard_map/factor/pallas_call | solution.py:161
  53.7 0.0 collective-permute-done.x1_ref
  53.7 0.1 collective-permute-start.1
  53.8 1.3 %finish.1 = (f32[4,32,32]{2,1,0:T(8,128)}, f32[128,128]{1,0:T(8,128)S(1)}) custom-call(f32[8,128]{1,0:T(8,128)S(1)} %get-tuple-element.31.tau8_ref, f32[128,128]{1,0:T(8,128)S(1)} %get-tuple-element.30.rit_ref, f32[128,128]{1,0:T(8,128)S(1)} %get-tuple-element.32.uit_ref, f32[128,128]{1,0:T(8,128)S(1)} %get-tuple-element.33.u_ref, ...), custom_call_target="tpu_custom_call" | custom-call | flops 300000000 | bytes 400000 | tf_op jit(solution)/shard_map/finish/pallas_call | solution.py:175
  55.0 0.2 collective-permute-done.1.x3_ref
  55.2 11.0 %update.1 = f32[1024,4096]{1,0:T(8,128)} custom-call(f32[8,1024,512]{2,1,0:T(8,128)S(1)} %get-tuple-element.21.a_ref, f32[8,4,32,512]{3,2,1,0:T(8,128)S(1)} %get-tuple-element.22.pt_ref, f32[512,128]{1,0:T(8,128)S(1)} %get-tuple-element.23.x0_ref, f32[512,128]{1,0:T(8,128)S(1)} %collective-permute-done.x1_ref, f32[512,128]{1,0:T(8,128)S(1)} %get-tuple-element.28.x2_ref, ...), custom_call_target="tpu_custom_call" | custom-call | tf_op jit(solution)/shard_map/update/pallas_call | solution.py:467
Async XLA Ops:
  44.9 8.8 %collective-permute-start = (f32[512,128]{1,0:T(8,128)S(1)}, f32[512,128]{1,0:T(8,128)S(1)}, u32[]{:S(2)}, u32[]{:S(2)}) collective-permute-start(f32[512,128]{1,0:T(8,128)S(1)} %get-tuple-element.23.x0_ref), channel_id=1, source_target_pairs={{0,2},{1,3},{2,0},{3,1},{4,6},{5,7},{6,4},{7,5},{8,10},{9,11},{10,... | collective-permute-start | bytes 786440 | tf_op jit(solution)/shard_map/ppermute | solution.py:487
  53.7 1.5 %collective-permute-start.1 = (f32[512,128]{1,0:T(8,128)S(1)}, f32[512,128]{1,0:T(8,128)S(1)}, u32[]{:S(2)}, u32[]{:S(2)}) collective-permute-start(f32[512,128]{1,0:T(8,128)S(1)} %collective-permute-done.x1_ref), channel_id=1, source_target_pairs={{0,1},{1,0},{2,3},{3,2},{4,5},{5,4},{6,7},{7,6},{8,9},{9,8},{10,11... | collective-permute-start | bytes 786440 | tf_op jit(solution)/shard_map/ppermute | solution.py:490

commit v9 on v8

--- a/solution.py
+++ b/solution.py
@@ -11,6 +11,7 @@
 NC = PANELS * BW
 CH = 512
 UPDATE_VMEM = 32 * 1024 * 1024
+WIDE = 2
 GATHER_VMEM = 32 * 1024 * 1024
 HIGHEST = lax.Precision.HIGHEST
 MESH = pl.DeviceIdType.MESH
@@ -439,23 +440,25 @@
 
     copies = []
     for step, strip in enumerate(strips):
-        wide = stack6(pt_ref[step].reshape(NC, CH), 0, RIGHT)
-        parts = 2 if step == len(strips) - 1 else 1
+        wide = [stack6(pt_ref[step * WIDE + i].reshape(NC, CH), 0, RIGHT) for i in range(WIDE)]
+        parts = 4 if step == len(strips) - 1 else 2
         size = ncol // parts
         for part in range(parts):
             lo = part * size
-            prod = lax.dot_general(z_v[lo:lo + size, :], wide, (((1,), (0,)), ((), ())), preferred_element_type=jnp.float32)
-            if part == 0:
-                new = jnp.concatenate([-prod[0:BW], a_ref[step, BW:size, :] - prod[BW:]], axis=0)
-            else:
-                new = a_ref[step, lo:lo + size, :] - prod
-            if step == 0:
-                strip[:, 0:NC] = jnp.where(r == 0, top_v[...], new[:, 0:NC])
-                strip[:, NC:] = new[:, NC:]
-            else:
-                strip[lo:lo + size, :] = new
+            for i in range(WIDE):
+                prod = lax.dot_general(z_v[lo:lo + size, :], wide[i], (((1,), (0,)), ((), ())), preferred_element_type=jnp.float32)
+                src = step * WIDE + i
+                if part == 0:
+                    new = jnp.concatenate([-prod[0:BW], a_ref[src, BW:size, :] - prod[BW:]], axis=0)
+                else:
+                    new = a_ref[src, lo:lo + size, :] - prod
+                if src == 0:
+                    strip[lo:lo + size, 0:NC] = jnp.where(r == 0, top_v[lo:lo + size, :], new[:, 0:NC])
+                    strip[lo:lo + size, NC:CH] = new[:, NC:]
+                else:
+                    strip[lo:lo + size, i * CH:(i + 1) * CH] = new
             copies.append(pltpu.make_async_copy(
-                strip.at[pl.ds(lo, size)], out_ref.at[pl.ds(lo, size), pl.ds(step * CH, CH)], sem.at[len(copies)]))
+                strip.at[pl.ds(lo, size)], out_ref.at[pl.ds(lo, size), pl.ds(step * WIDE * CH, WIDE * CH)], sem.at[len(copies)]))
             copies[-1].start()
     for copy in copies:
         copy.wait()
@@ -469,8 +472,8 @@
         out_shape=jax.ShapeDtypeStruct((ncol, nch * CH), jnp.float32),
         in_specs=[vm] * 11,
         out_specs=pl.BlockSpec(memory_space=pl.ANY),
-        scratch_shapes=[pltpu.VMEM((ncol, 6 * NC), jnp.bfloat16), pltpu.VMEM((ncol, NC), jnp.float32), pltpu.SemaphoreType.DMA((nch + 1,))]
-        + [pltpu.VMEM((ncol, CH), jnp.float32)] * nch,
+        scratch_shapes=[pltpu.VMEM((ncol, 6 * NC), jnp.bfloat16), pltpu.VMEM((ncol, NC), jnp.float32), pltpu.SemaphoreType.DMA((2 * nch,))]
+        + [pltpu.VMEM((ncol, WIDE * CH), jnp.float32)] * (nch // WIDE),
         compiler_params=pltpu.CompilerParams(vmem_limit_bytes=UPDATE_VMEM),
         name="update",
     )(a, pt, *xs, head, rit, nmat, uit, facet)

time: 66.5 us -> 64.6 us (0.971)
  Pallas kernels: 63.7 us -> 61.8 us
    pallas_call x1, Pallas kernels: 11 us -> 9.1 us  [update(): pl.pallas_call(update_kernel, out_shape=jax.ShapeDtypeStruct((ncol, nch *...]
where the time goes in v9:
time: 64.6 us; the launch traced here: 64.5 us
  Pallas kernels  61.8 us (96%)
  starting transfers between devices  1.67 us (3%)
  between operations  0.8 us (1%)
    pallas_call x1, Pallas kernels, gather(): pl.pallas_call(gather_kernel, out_shape=(jax.ShapeDtypeStruct((nch, ncol,...  44.2 us
    pallas_call x1, Pallas kernels, update(): pl.pallas_call(update_kernel, out_shape=jax.ShapeDtypeStruct((ncol, nch *...  9.1 us
    pallas_call x1, Pallas kernels, factor(): pl.pallas_call(factor_kernel, out_shape=(sq, tau, jax.ShapeDtypeStruct((8...  7.22 us
    ppermute x1, starting transfers between devices, device_fn(): x1 = lax.ppermute(xh, 'row', [(i, i ^ 2) for i in range(4)])  1.59 us
  transfers between devices with their start and end apart: 2, of which 1 were waited for; matrix products, arithmetic and copies ran while one was open for 0% of the time, Pallas kernels for 13%

profile of v9, /device:TPU:0, one launch (start us, length us, event | category | flops | bytes accessed | tf_op | source)
XLA Modules:
  0.0 64.5 jit_solution(9450340972771691039)
XLA Ops:
  0.6 44.2 %gather.1 = (f32[8,1024,512]{2,1,0:T(8,128)S(1)}, f32[8,4,32,512]{3,2,1,0:T(8,128)S(1)}, f32[512,128]{1,0:T(8,128)S(1)}, f32[512,128]{1,0:T(8,128)S(1)}, f32[128...) custom-call(f32[1024,4096]{1,0:T(8,128)} %bitcast.7), custom_call_target="tpu_custom_call" | custom-call | tf_op jit(solution)/shard_map/gather/pallas_call | solution.py:407
  44.9 1.6 %collective-permute-start = (f32[512,128]{1,0:T(8,128)S(1)}, f32[512,128]{1,0:T(8,128)S(1)}, u32[]{:S(2)}, u32[]{:S(2)}) collective-permute-start(f32[512,128]{1,0:T(8,128)S(1)} %get-tuple-element.23.x0_ref), channel_id=1, source_target_pairs={{0,2},{1,3},{2,0},{3,1},{4,6},{5,7},{6,4},{7,5},{8,10},{9,11},{10,... | collective-permute-start | bytes 786440 | tf_op jit(solution)/shard_map/ppermute | solution.py:490
  46.5 7.2 %factor.1 = (f32[128,128]{1,0:T(8,128)S(1)}, f32[1,128]{1,0:T(1,128)}, f32[8,128]{1,0:T(8,128)S(1)}, f32[128,128]{1,0:T(8,128)S(1)}, f32[128,128]{1,0:T(8,128)S(...) custom-call(f32[128,128]{1,0:T(8,128)S(1)} %get-tuple-element.24.g_ref, f32[128,128]{1,0:T(8,128)S(1)} %get-tuple-element.25.ptop_ref), custom_call_target="tpu_custom_call" | custom-call | flops 1000000000 | bytes 600000 | tf_op jit(solution)/shard_map/factor/pallas_call | solution.py:162
  53.7 0.0 collective-permute-done.x1_ref
  53.7 0.1 collective-permute-start.1
  53.8 1.3 %finish.1 = (f32[4,32,32]{2,1,0:T(8,128)}, f32[128,128]{1,0:T(8,128)S(1)}) custom-call(f32[8,128]{1,0:T(8,128)S(1)} %get-tuple-element.31.tau8_ref, f32[128,128]{1,0:T(8,128)S(1)} %get-tuple-element.30.rit_ref, f32[128,128]{1,0:T(8,128)S(1)} %get-tuple-element.32.uit_ref, f32[128,128]{1,0:T(8,128)S(1)} %get-tuple-element.33.u_ref, ...), custom_call_target="tpu_custom_call" | custom-call | flops 300000000 | bytes 400000 | tf_op jit(solution)/shard_map/finish/pallas_call | solution.py:176
  55.0 0.2 collective-permute-done.1.x3_ref
  55.2 9.1 %update.1 = f32[1024,4096]{1,0:T(8,128)} custom-call(f32[8,1024,512]{2,1,0:T(8,128)S(1)} %get-tuple-element.21.a_ref, f32[8,4,32,512]{3,2,1,0:T(8,128)S(1)} %get-tuple-element.22.pt_ref, f32[512,128]{1,0:T(8,128)S(1)} %get-tuple-element.23.x0_ref, f32[512,128]{1,0:T(8,128)S(1)} %collective-permute-done.x1_ref, f32[512,128]{1,0:T(8,128)S(1)} %get-tuple-element.28.x2_ref, ...), custom_call_target="tpu_custom_call" | custom-call | tf_op jit(solution)/shard_map/update/pallas_call | solution.py:470
Async XLA Ops:
  44.9 8.8 %collective-permute-start = (f32[512,128]{1,0:T(8,128)S(1)}, f32[512,128]{1,0:T(8,128)S(1)}, u32[]{:S(2)}, u32[]{:S(2)}) collective-permute-start(f32[512,128]{1,0:T(8,128)S(1)} %get-tuple-element.23.x0_ref), channel_id=1, source_target_pairs={{0,2},{1,3},{2,0},{3,1},{4,6},{5,7},{6,4},{7,5},{8,10},{9,11},{10,... | collective-permute-start | bytes 786440 | tf_op jit(solution)/shard_map/ppermute | solution.py:490
  53.7 1.5 %collective-permute-start.1 = (f32[512,128]{1,0:T(8,128)S(1)}, f32[512,128]{1,0:T(8,128)S(1)}, u32[]{:S(2)}, u32[]{:S(2)}) collective-permute-start(f32[512,128]{1,0:T(8,128)S(1)} %collective-permute-done.x1_ref), channel_id=1, source_target_pairs={{0,1},{1,0},{2,3},{3,2},{4,5},{5,4},{6,7},{7,6},{8,9},{9,8},{10,11... | collective-permute-start | bytes 786440 | tf_op jit(solution)/shard_map/ppermute | solution.py:493
